TPU v7x, 32 devices: a whole 2x2x4 slice. The times are simulated.
32 devices in a mesh: groups: 2 (over y), seq: 4 (over z), rep: 4 (over x, core).
Axes of the slice: x: 2, y: 2, z: 4, core: 2. Of those that a mesh axis runs over, the one named last changes fastest.
Arguments:
- queries: bfloat16 [128, 2048], P(('groups', 'seq'), 'rep'), parts along dimension 0, may hold values from -128 to 128
- keys_new: bfloat16 [128, 512], P(('groups', 'seq'), 'rep'), parts along dimension 0, may hold values from -4 to 4
- values_new: bfloat16 [128, 512], P(('groups', 'seq'), 'rep'), parts along dimension 0, may hold values from -6 to 6
- keys_past: bfloat16 [2048, 512], P(('groups', 'seq'), 'rep'), parts along dimension 0, may hold values from -4 to 4
- values_past: bfloat16 [2048, 512], P(('groups', 'seq'), 'rep'), parts along dimension 0, may hold values from -6 to 6
- block_order: int32 [8], P('groups'), parts along dimension 0, may hold values from 0 to 3, each once
- residual: bfloat16 [128, 4096], P(('groups', 'seq'), 'rep'), parts along dimension 0, may hold values from -6 to 6
- out_proj: bfloat16 [2048, 4096], P('seq', 'rep'), may hold values from -0.125 to 0.125
- norm_gain: float32 [4096], replicated, may hold values from 0.5 to 1.5
- router: float32 [4096, 4], replicated, may hold values from -0.09375 to 0.09375
- w_gate: bfloat16 [4, 4096, 8192], P('rep', None, 'seq'), may hold values from -0.09375 to 0.09375
- w_up: bfloat16 [4, 4096, 8192], P('rep', None, 'seq'), may hold values from -0.09375 to 0.09375
- w_down: bfloat16 [4, 8192, 4096], P('rep', 'seq'), may hold values from -0.0625 to 0.0625
- expert_ids: int32 [128, 2], P(('groups', 'seq')), parts along dimension 0, may hold values from 0 to 3, all different within a row; in each aligned block of 16 rows (0 to 15, 16 to 31, ...) at most 12 rows name the same one
Outputs:
- attended: bfloat16 [128, 4096], P(('groups', 'seq'), 'rep'), parts along dimension 0
- layer_out: bfloat16 [128, 4096], P(('groups', 'seq'), 'rep'), parts along dimension 0
- keys_cache: bfloat16 [128, 512], P(('groups', 'seq')), parts along dimension 0
- values_cache: bfloat16 [128, 512], P(('groups', 'seq')), parts along dimension 0
There are 2 independent parts, one for each index of `groups`. A program takes and returns all parts, laid end to end along the dimension named above; an argument that names none is the same for every part. Nothing has to cross between parts.
Inputs may be any that keep to these rules, and one draw needn't show every extreme that they name: `block_order`: each block index 0 to 4 - 1 appears once. `expert_ids`: each row names 2 different experts; in the rows of one device (aligned blocks of 16 rows) no expert is named by more than 12 rows, and in some block one expert is named by exactly 12.
All inputs are finite; a program needn't handle non-finite values.
Results may differ from a plain program's by a relative error of at most 0.011.
Values may be sent and summed in bfloat16 or wider, within the bound.
A program may use at most 128 MiB of HBM per device.

v0:
```python
import functools
import math

import jax
import jax.numpy as jnp
from jax import lax
from jax.experimental import pallas as pl
from jax.experimental.pallas import tpu as pltpu
from jax.sharding import PartitionSpec as P

EXPERTS = 4
CAP = 12


def block_lookup(owners, block_order):
    width = block_order.shape[0]
    hits = owners[:, None] == jnp.arange(width, dtype=jnp.int32)[None, :]
    return jnp.sum(jnp.where(hits, block_order[None, :], 0), axis=1)


def plain_body(
    queries,
    keys_new,
    values_new,
    keys_past,
    values_past,
    block_order,
    residual,
    out_proj,
    norm_gain,
    router,
    w_gate,
    w_up,
    w_down,
    expert_ids,
):
    seq_index = lax.axis_index("seq")
    rep_index = lax.axis_index("rep")
    rep_count = lax.axis_size("rep")
    tok_count = queries.shape[0]
    head_dim = keys_new.shape[1]
    q_per = queries.shape[1] // head_dim
    past_len = keys_past.shape[0]
    key_span = past_len + tok_count
    row_total = tok_count * q_per
    my_block = block_lookup(jnp.full((1,), seq_index, jnp.int32), block_order)[0]
    scaling = 1.0 / math.sqrt(head_dim)
    query_rows = queries.reshape(row_total, head_dim)
    query_pos = my_block * tok_count + jnp.arange(row_total, dtype=jnp.int32) // q_per
    keys_local = jnp.concatenate([keys_past, keys_new], axis=0)
    values_local = jnp.concatenate([values_past, values_new], axis=0)
    running = jnp.full((row_total,), -1e30, jnp.float32)
    key_piece = lax.all_gather(keys_local, "seq", axis=0, tiled=True)
    value_piece = lax.all_gather(values_local, "seq", axis=0, tiled=True)
    row_count = key_piece.shape[0]
    key_index = jnp.arange(row_count, dtype=jnp.int32)
    key_owner = key_index // key_span
    offset = key_index % key_span
    key_pos = block_lookup(key_owner, block_order) * tok_count + offset - past_len
    visible = (offset < past_len)[None, :] | (key_pos[None, :] <= query_pos[:, None])
    scores = jnp.dot(query_rows, key_piece.T, preferred_element_type=jnp.float32) * scaling
    highest = jnp.maximum(running, jnp.max(jnp.where(visible, scores, -1e30), axis=1))
    weights = jnp.where(visible, jnp.exp(scores - highest[:, None]), 0.0)
    totals = jnp.sum(weights, axis=1)
    numerator = jnp.dot(
        weights.astype(jnp.bfloat16), value_piece, preferred_element_type=jnp.float32
    )
    running, totals, numerator = (highest, totals, numerator)
    attn_local = (
        (numerator / totals[:, None]).reshape(tok_count, q_per * head_dim).astype(jnp.bfloat16)
    )
    attn_full, keys_cache, values_cache = (
        lax.all_gather(attn_local, "rep", axis=1, tiled=True),
        lax.all_gather(keys_new, "rep", axis=1, tiled=True),
        lax.all_gather(values_new, "rep", axis=1, tiled=True),
    )
    head_rows = lax.all_to_all(attn_full, "seq", split_axis=1, concat_axis=0, tiled=True)
    projected = lax.psum_scatter(
        jnp.dot(head_rows, out_proj, preferred_element_type=jnp.float32).astype(jnp.bfloat16),
        "seq",
        scatter_dimension=0,
        tiled=True,
    ).astype(jnp.float32)
    attended = (residual.astype(jnp.float32) + projected).astype(jnp.bfloat16)
    full_rows = lax.all_gather(attended, "rep", axis=1, tiled=True)
    features = full_rows.astype(jnp.float32)
    mean_square = jnp.mean(features * features, axis=1, keepdims=True)
    normed = (features * norm_gain[None, :] * lax.rsqrt(mean_square + 1e-05)).astype(jnp.bfloat16)
    logits = jnp.dot(normed.astype(jnp.float32), router, precision=lax.Precision.HIGHEST)
    expert_range = jnp.arange(EXPERTS, dtype=jnp.int32)
    first_pick = (expert_ids[:, 0:1] == expert_range[None, :]).astype(jnp.float32)
    second_pick = (expert_ids[:, 1:2] == expert_range[None, :]).astype(jnp.float32)
    share_first = jax.nn.sigmoid(
        jnp.sum(first_pick * logits, axis=1) - jnp.sum(second_pick * logits, axis=1)
    )
    token_share = share_first[:, None] * first_pick + (1.0 - share_first)[:, None] * second_pick
    member = first_pick + second_pick
    ranking = jnp.cumsum(member, axis=0) - member
    slot_range = jnp.arange(CAP, dtype=jnp.float32)
    selection = member.T[:, None, :] * (ranking.T[:, None, :] == slot_range[None, :, None]).astype(
        jnp.float32
    )
    mine_mask = (expert_range == rep_index % EXPERTS).astype(jnp.float32)
    my_selection = jnp.einsum("e,ejt->jt", mine_mask, selection)
    slot_rows = jnp.dot(
        my_selection.astype(jnp.bfloat16), normed, preferred_element_type=jnp.float32
    ).astype(jnp.bfloat16)
    gate_local = w_gate[0]
    up_local = w_up[0]
    down_local = w_down[0]
    piece = lax.all_gather(slot_rows, "seq", axis=0, tiled=True)
    gate_part = jnp.dot(piece, gate_local, preferred_element_type=jnp.float32)
    up_part = jnp.dot(piece, up_local, preferred_element_type=jnp.float32)
    hidden_slots = (jax.nn.silu(gate_part) * up_part).astype(jnp.bfloat16)
    expert_part = lax.psum_scatter(
        jnp.dot(hidden_slots, down_local, preferred_element_type=jnp.float32).astype(jnp.bfloat16),
        "seq",
        scatter_dimension=0,
        tiled=True,
    ).astype(jnp.float32)
    returned = lax.all_to_all(
        expert_part.astype(jnp.bfloat16), "rep", split_axis=1, concat_axis=0, tiled=True
    ).astype(expert_part.dtype)
    source_expert = jnp.arange(rep_count, dtype=jnp.int32) % EXPERTS
    source_pick = (source_expert[:, None] == expert_range[None, :]).astype(jnp.float32)
    combine = jnp.einsum("re,ejt,te->trj", source_pick, selection, token_share).reshape(
        tok_count, rep_count * CAP
    )
    moe_slice = jnp.dot(combine, returned, precision=lax.Precision.HIGHEST)
    layer_out = (attended.astype(jnp.float32) + moe_slice).astype(jnp.bfloat16)
    return (attended, layer_out, keys_cache, values_cache)


MESH = pl.DeviceIdType.MESH
STAT_ROWS = 8
F32 = jnp.float32
BF16 = jnp.bfloat16


def fused_kernel(
    n_seq,
    n_rep,
    order_ref,
    q_ref,
    kn_ref,
    vn_ref,
    kp_ref,
    vp_ref,
    res_ref,
    gain_ref,
    router_ref,
    ids_ref,
    proj_hbm,
    gate_hbm,
    up_hbm,
    down_hbm,
    att_out,
    layer_out,
    kc_out,
    vc_out,
    wproj,
    wgate,
    wup,
    wdown,
    qall,
    idall,
    kcache,
    vcache,
    num_send,
    stat_send,
    num_all,
    stat_all,
    part_send,
    part_all,
    xall,
    gained,
    gate_acc,
    up_acc,
    inverse_ref,
    hidden,
    ysend,
    yall,
    zsend,
    zall,
    w_sem,
    small_send,
    small_recv,
    num_ssem,
    num_rsem,
    hand_ssem,
    pass_ssem,
    pass_rsem,
    part_ssem,
    part_rsem,
    x_ssem,
    x_rsem,
    y_ssem,
    y_rsem,
    z_ssem,
    z_rsem,
):
    group = lax.axis_index("groups")
    seq = lax.axis_index("seq")
    rep = lax.axis_index("rep")
    tok, width = q_ref.shape
    hd = kn_ref.shape[1]
    q_per = width // hd
    toks = tok * n_seq
    feat = res_ref.shape[1]

    chips = n_rep // 2
    chip, core = rep // 2, lax.rem(rep, 2)
    partner = chip * 2 + 1 - core

    def same_core(step):
        return lax.rem(chip + step, chips) * 2 + core

    def other_core(step):
        return lax.rem(chip + step, chips) * 2 + 1 - core

    def dev(s, r):
        return {"groups": group, "seq": s, "rep": r}

    def other(index, step, size):
        return lax.rem(index + step, size)

    def remote(src, dst, ssem, rsem, s, r):
        return pltpu.make_async_remote_copy(
            src_ref=src,
            dst_ref=dst,
            send_sem=ssem,
            recv_sem=rsem,
            device_id=dev(s, r),
            device_id_type=MESH,
        )

    def rows_of(index):
        return pl.ds(pl.multiple_of(index * tok, tok), tok)

    loads = []
    for i, (src, dst) in enumerate(
        ((proj_hbm, wproj), (gate_hbm.at[0], wgate), (up_hbm.at[0], wup), (down_hbm.at[0], wdown))
    ):
        pieces = 1 if i == 0 else 4
        size = dst.shape[0] // pieces
        for j in range(pieces):
            span = pl.ds(j * size, size)
            load = pltpu.make_async_copy(src.at[span], dst.at[span], w_sem.at[i, j])
            load.start()
            loads.append(load)

    barrier = pltpu.get_barrier_semaphore()
    for i in range(n_seq):
        for j in range(n_rep):
            if i or j:
                pl.semaphore_signal(
                    barrier,
                    inc=1,
                    device_id=dev(other(seq, i, n_seq), other(rep, j, n_rep)),
                    device_id_type=MESH,
                )
    lane = lax.broadcasted_iota(jnp.int32, (tok, 128), 1)
    ids_f = ids_ref[...].astype(F32)
    diagonal = lax.broadcasted_iota(jnp.int32, (tok, tok), 0) == lax.broadcasted_iota(
        jnp.int32, (tok, tok), 1
    )
    picks = [
        jnp.sum(jnp.where(diagonal, ids_f[i : i + 1, :], 0.0), axis=1, keepdims=True)
        for i in range(2)
    ]
    idall[rows_of(seq), :] = jnp.where(lane == 0, picks[0], picks[1])
    qall[rows_of(seq), :] = q_ref[...]
    for j in range(n_rep):

        @pl.when(rep == j)
        def _():
            kcache[:, j * hd : (j + 1) * hd] = kn_ref[...]
            vcache[:, j * hd : (j + 1) * hd] = vn_ref[...]

    pl.semaphore_wait(barrier, n_seq * n_rep - 1)

    sends = []

    def send(copy):
        copy.start()
        sends.append(copy)

    for k in range(1, n_seq):
        to = other(seq, k, n_seq)
        mine = rows_of(seq)
        send(remote(q_ref, qall.at[mine], small_send.at[0, k], small_recv.at[0, seq], to, rep))
    for k in range(1, n_seq):
        to = other(seq, k, n_seq)
        mine = rows_of(seq)
        send(
            remote(idall.at[mine], idall.at[mine], small_send.at[1, k], small_recv.at[1, seq], to, rep)
        )

    own_pos = order_ref[seq] * tok + lax.broadcasted_iota(jnp.int32, (tok, tok), 1)
    bias = [
        jnp.where(
            own_pos <= order_ref[t] * tok + lax.broadcasted_iota(jnp.int32, (tok, tok), 0),
            0.0,
            -1e30,
        )
        for t in range(n_seq)
    ]
    bias = jnp.concatenate(bias * q_per, axis=0)

    for k in range(1, n_seq):
        frm = other(seq, k, n_seq)
        src = rows_of(frm)
        remote(q_ref, qall.at[src], small_send.at[0, k], small_recv.at[0, frm], frm, rep).wait_recv()

    scaling = 1.0 / math.sqrt(hd)
    queries = jnp.concatenate([qall[:, h * hd : (h + 1) * hd] for h in range(q_per)], axis=0)
    nt = (((1,), (1,)), ((), ()))
    s_past = lax.dot_general(queries, kp_ref[...], nt, preferred_element_type=F32) * scaling
    s_new = lax.dot_general(queries, kn_ref[...], nt, preferred_element_type=F32) * scaling + bias
    high = jnp.maximum(
        jnp.max(s_past, axis=1, keepdims=True), jnp.max(s_new, axis=1, keepdims=True)
    )
    w_past = jnp.exp(s_past - high)
    w_new = jnp.exp(s_new - high)
    total = jnp.sum(w_past, axis=1, keepdims=True) + jnp.sum(w_new, axis=1, keepdims=True)
    num = jnp.dot(w_past.astype(BF16), vp_ref[...], preferred_element_type=F32) + jnp.dot(
        w_new.astype(BF16), vn_ref[...], preferred_element_type=F32
    )
    rows = num.shape[0]
    stat_lane = lax.broadcasted_iota(jnp.int32, (rows, 128), 1)
    stats = jnp.where(stat_lane == 0, high, total)
    stat_send[...] = stats.T[:STAT_ROWS, :]
    num_send[...] = num.astype(BF16)

    stat_rows = pl.ds(pl.multiple_of(seq * STAT_ROWS, STAT_ROWS), STAT_ROWS)

    def partial_copies(k):
        to = same_core(k)
        return (
            remote(num_send, num_all.at[seq], num_ssem.at[0, k], num_rsem.at[0, seq], rep, to),
            remote(
                stat_send, stat_all.at[stat_rows], num_ssem.at[1, k], num_rsem.at[1, seq], rep, to
            ),
        )

    for k in range(1, chips):
        for copy in partial_copies(k):
            send(copy)

    @pl.when(seq != rep)
    def _():
        for copy in partial_copies(0):
            copy.start()

    @pl.when(seq == rep)
    def _():
        num_all[seq] = num_send[...]
        stat_all[stat_rows, :] = stat_send[...]

    for j in range(n_rep):

        @pl.when(rep == j)
        def _():
            cols = pl.ds(j * hd, hd)
            for k in range(1, n_rep):
                to = (j + k) % n_rep
                remote(
                    kn_ref, kcache.at[:, cols], small_send.at[2, k], small_recv.at[2, j], seq, to
                ).start()
                remote(
                    vn_ref, vcache.at[:, cols], small_send.at[3, k], small_recv.at[3, j], seq, to
                ).start()

    def wait_partial(frm):
        src_rows = pl.ds(pl.multiple_of(frm * STAT_ROWS, STAT_ROWS), STAT_ROWS)
        remote(
            num_send, num_all.at[frm], num_ssem.at[0, 0], num_rsem.at[0, frm], seq, rep
        ).wait_recv()
        remote(
            stat_send, stat_all.at[src_rows], num_ssem.at[1, 0], num_rsem.at[1, frm], seq, rep
        ).wait_recv()

    def handed(frm):
        src_rows = pl.ds(pl.multiple_of(frm * STAT_ROWS, STAT_ROWS), STAT_ROWS)
        return (
            remote(
                num_all.at[frm], num_all.at[frm], hand_ssem.at[0, frm], num_rsem.at[0, frm], seq, partner
            ),
            remote(
                stat_all.at[src_rows],
                stat_all.at[src_rows],
                hand_ssem.at[1, frm],
                num_rsem.at[1, frm],
                seq,
                partner,
            ),
        )

    first_core = lax.rem(seq, 2)

    @pl.when(core == first_core)
    def _():
        @pl.when(seq == rep)
        def _():
            for copy in handed(seq):
                copy.start()

        for k in range(1, n_seq):
            frm = other(seq, k, n_seq)
            wait_partial(frm)
            for copy in handed(frm):
                copy.start()

        @pl.when(seq != rep)
        def _():
            wait_partial(seq)
            for copy in handed(seq):
                copy.start()

    @pl.when(core != first_core)
    def _():
        for k in range(n_seq):
            wait_partial(other(seq, k, n_seq))

    @pl.when(seq != rep)
    def _():
        for copy in partial_copies(0):
            copy.wait_send()

    stat_cols = jnp.concatenate(
        [stat_all[...], jnp.zeros((128 - n_seq * STAT_ROWS, rows), F32)], axis=0
    ).T
    highs = [stat_cols[:, s * STAT_ROWS : s * STAT_ROWS + 1] for s in range(n_seq)]
    top = functools.reduce(jnp.maximum, highs)
    scales = [jnp.exp(h - top) for h in highs]
    full = sum(
        scales[s] * stat_cols[:, s * STAT_ROWS + 1 : s * STAT_ROWS + 2] for s in range(n_seq)
    )
    heads = sum(scales[s] * num_all[s].astype(F32) for s in range(n_seq)) / full
    heads = heads.astype(BF16)
    head_rows = jnp.concatenate([heads[h * toks : (h + 1) * toks] for h in range(q_per)], axis=1)
    loads[0].wait()
    part_send[...] = jnp.dot(head_rows, wproj[...], preferred_element_type=F32).astype(BF16)
    for k in range(1, n_seq):
        to = other(seq, k, n_seq)
        send(
            remote(
                part_send.at[rows_of(to)], part_all.at[seq], part_ssem.at[k], part_rsem.at[seq], to, rep
            )
        )
    projected = part_send[rows_of(seq), :].astype(F32)
    for k in range(1, n_seq):
        frm = other(seq, k, n_seq)
        remote(
            part_send.at[rows_of(frm)], part_all.at[frm], part_ssem.at[k], part_rsem.at[frm], frm, rep
        ).wait_recv()
        projected = projected + part_all[frm].astype(F32)
    attended = (res_ref[...].astype(F32) + projected).astype(BF16)
    att_out[...] = attended
    xall[rep, rows_of(seq), :] = attended

    def x_copy(r, s, slot, to_s, to_r):
        view = xall.at[r, rows_of(s)]
        return remote(view, view, x_ssem.at[slot[0], slot[1]], x_rsem.at[r, s], to_s, to_r)

    for k in range(1, n_seq):
        send(x_copy(rep, seq, (0, k), other(seq, k, n_seq), rep))
    def spread(frm, k):
        for j in range(1, chips):
            send(x_copy(rep, frm, (1 + j, k), seq, same_core(j)))
        send(x_copy(rep, frm, (1, k), seq, partner))

    spread(seq, 0)
    for k in range(1, n_seq):
        frm = other(seq, n_seq - k, n_seq)
        x_copy(rep, frm, (0, k), frm, rep).wait_recv()
        spread(frm, k)

    def quarter_wait(at):
        for k in range(n_seq):
            x_copy(at, other(seq, n_seq - k, n_seq), (1, k), seq, at).wait_recv()

    for load in loads[1:9]:
        load.wait()
    hidden_width = wgate.shape[1]
    chunk = min(512, hidden_width)

    def scaled_quarter(at):
        cols = pl.ds(pl.multiple_of(at * feat, feat), feat)
        part = xall[at].astype(F32)
        gained[...] = (part * gain_ref[:, cols]).astype(BF16)
        return jnp.sum(part * part, axis=1, keepdims=True)

    def products(at, cols):
        span = pl.ds(pl.multiple_of(at * feat, feat), feat)
        return (
            jnp.dot(gained[...], wgate[span, cols], preferred_element_type=F32),
            jnp.dot(gained[...], wup[span, cols], preferred_element_type=F32),
        )

    def add_quarter(at, start):
        @pl.loop(0, hidden_width // chunk)
        def _(c):
            cols = pl.ds(pl.multiple_of(c * chunk, chunk), chunk)
            gate, up = products(at, cols)
            if start:
                gate_acc[:, cols] = gate
                up_acc[:, cols] = up
            else:
                gate_acc[:, cols] += gate
                up_acc[:, cols] += up

    squares = scaled_quarter(rep)
    add_quarter(rep, True)
    quarter_wait(partner)
    squares = squares + scaled_quarter(partner)
    add_quarter(partner, False)
    for j in range(1, chips):
        at = same_core(j)
        quarter_wait(at)
        send(remote(xall.at[at], xall.at[at], pass_ssem.at[j], pass_rsem.at[j], seq, partner))
        squares = squares + scaled_quarter(at)
        add_quarter(at, False)
    for j in range(1, chips):
        at = other_core(j)
        remote(
            xall.at[at], xall.at[at], pass_ssem.at[j], pass_rsem.at[j], seq, partner
        ).wait_recv()
        squares = squares + scaled_quarter(at)
        if j < chips - 1:
            add_quarter(at, False)
    last = other_core(chips - 1)
    inverse = lax.rsqrt(squares / (feat * n_rep) + 1e-05)
    inverse_ref[...] = jnp.broadcast_to(inverse, (toks, 128))

    @pl.loop(0, hidden_width // chunk)
    def _(c):
        cols = pl.ds(pl.multiple_of(c * chunk, chunk), chunk)
        factor = inverse_ref[:, 0:1]
        gate, up = products(last, cols)
        gate = (gate_acc[:, cols] + gate) * factor
        up = (up_acc[:, cols] + up) * factor
        hidden[:, cols] = (gate * jax.nn.sigmoid(gate) * up).astype(BF16)

    for load in loads[9:]:
        load.wait()
    targets = [f(j) for j in range(1, chips) for f in (same_core, other_core)]
    targets = list(enumerate(targets + [partner], 1)) + [(0, rep)]
    for k, to in targets:
        cols = pl.ds(pl.multiple_of(to * feat, feat), feat)
        product = jnp.dot(hidden[...], wdown[:, cols], preferred_element_type=F32).astype(BF16)
        if k:
            ysend[k - 1] = product
            send(remote(ysend.at[k - 1], yall.at[rep], y_ssem.at[k], y_rsem.at[rep], seq, to))
        else:
            yall[rep] = product

    for k in range(1, n_seq):
        frm = other(seq, k, n_seq)
        src = rows_of(frm)
        remote(
            idall.at[src], idall.at[src], small_send.at[1, k], small_recv.at[1, frm], frm, rep
        ).wait_recv()
    experts = router_ref.shape[0]
    logits = [jnp.zeros((toks, 1), F32) for _ in range(experts)]
    for j in range(n_rep):
        cols = slice(j * feat, (j + 1) * feat)
        part = (xall[j].astype(F32) * gain_ref[:, cols] * inverse).astype(BF16).astype(F32)
        for e in range(experts):
            logits[e] = logits[e] + jnp.sum(part * router_ref[e : e + 1, cols], axis=1, keepdims=True)
    first = [(idall[:, 0:1] == float(e)).astype(F32) for e in range(experts)]
    second = [(idall[:, 1:2] == float(e)).astype(F32) for e in range(experts)]
    gap = sum(first[e] * logits[e] for e in range(experts)) - sum(
        second[e] * logits[e] for e in range(experts)
    )
    share = jax.nn.sigmoid(gap)
    shares = [share * first[e] + (1.0 - share) * second[e] for e in range(experts)]

    for k in range(1, n_rep):
        frm = other(rep, k, n_rep)
        remote(ysend.at[0], yall.at[frm], y_ssem.at[k], y_rsem.at[frm], seq, frm).wait_recv()
    mixture = sum(shares[j % experts] * yall[j].astype(F32) for j in range(n_rep))
    zsend[...] = mixture.astype(BF16)
    for k in range(1, n_seq):
        to = other(seq, k, n_seq)
        send(remote(zsend.at[rows_of(to)], zall.at[seq], z_ssem.at[k], z_rsem.at[seq], to, rep))
    for j in range(n_rep):

        @pl.when(rep != j)
        def _():
            cols = pl.ds(j * hd, hd)
            remote(
                kn_ref, kcache.at[:, cols], small_send.at[2, 0], small_recv.at[2, j], seq, rep
            ).wait_recv()
            remote(
                vn_ref, vcache.at[:, cols], small_send.at[3, 0], small_recv.at[3, j], seq, rep
            ).wait_recv()

    kc_out[...] = kcache[...]
    vc_out[...] = vcache[...]
    result = xall[rep, rows_of(seq), :].astype(F32) + zsend[rows_of(seq), :].astype(F32)
    for k in range(1, n_seq):
        frm = other(seq, k, n_seq)
        remote(
            zsend.at[rows_of(frm)], zall.at[frm], z_ssem.at[k], z_rsem.at[frm], frm, rep
        ).wait_recv()
        result = result + zall[frm].astype(F32)
    layer_out[...] = result.astype(BF16)

    for copy in sends:
        copy.wait_send()

    @pl.when(core == first_core)
    def _():
        for s in range(n_seq):
            for copy in handed(s):
                copy.wait_send()

    for k in range(1, n_rep):
        for which, src in ((2, kn_ref), (3, vn_ref)):
            remote(
                src,
                (kcache if which == 2 else vcache).at[:, pl.ds(0, hd)],
                small_send.at[which, k],
                small_recv.at[which, 0],
                seq,
                rep,
            ).wait_send()


def hand_over(*refs):
    for src, dst in zip(refs[:4], refs[4:]):
        dst[...] = src[...]


def fused_body(
    queries,
    keys_new,
    values_new,
    keys_past,
    values_past,
    block_order,
    residual,
    out_proj,
    norm_gain,
    router,
    w_gate,
    w_up,
    w_down,
    expert_ids,
):
    n_seq = lax.axis_size("seq")
    n_rep = lax.axis_size("rep")
    tok, width = queries.shape
    hd = keys_new.shape[1]
    toks = tok * n_seq
    rows = toks * (width // hd)
    feat = residual.shape[1]
    vmem = pl.BlockSpec(memory_space=pltpu.VMEM)
    smem = pl.BlockSpec(memory_space=pltpu.SMEM)
    hbm = pl.BlockSpec(memory_space=pl.ANY)
    dma = pltpu.SemaphoreType.DMA
    cache = (tok, hd * n_rep)
    outs = pl.pallas_call(
        functools.partial(fused_kernel, n_seq, n_rep),
        out_shape=(
            jax.ShapeDtypeStruct((tok, feat), BF16),
            jax.ShapeDtypeStruct((tok, feat), BF16),
            jax.ShapeDtypeStruct(cache, BF16),
            jax.ShapeDtypeStruct(cache, BF16),
        ),
        in_specs=[smem] + [vmem] * 9 + [hbm] * 4,
        out_specs=(vmem,) * 4,
        scratch_shapes=[
            pltpu.VMEM(out_proj.shape, BF16),
            pltpu.VMEM(w_gate.shape[1:], BF16),
            pltpu.VMEM(w_up.shape[1:], BF16),
            pltpu.VMEM(w_down.shape[1:], BF16),
            pltpu.VMEM((toks, width), BF16),
            pltpu.VMEM((toks, 128), F32),
            pltpu.VMEM(cache, BF16),
            pltpu.VMEM(cache, BF16),
            pltpu.VMEM((rows, hd), BF16),
            pltpu.VMEM((STAT_ROWS, rows), F32),
            pltpu.VMEM((n_seq, rows, hd), BF16),
            pltpu.VMEM((n_seq * STAT_ROWS, rows), F32),
            pltpu.VMEM((toks, feat), BF16),
            pltpu.VMEM((n_seq, tok, feat), BF16),
            pltpu.VMEM((n_rep, toks, feat), BF16),
            pltpu.VMEM((toks, feat), BF16),
            pltpu.VMEM((toks, w_gate.shape[2]), F32),
            pltpu.VMEM((toks, w_gate.shape[2]), F32),
            pltpu.VMEM((toks, 128), F32),
            pltpu.VMEM((toks, w_gate.shape[2]), BF16),
            pltpu.VMEM((n_rep - 1, toks, feat), BF16),
            pltpu.VMEM((n_rep, toks, feat), BF16),
            pltpu.VMEM((toks, feat), BF16),
            pltpu.VMEM((n_seq, tok, feat), BF16),
            dma((4, 4)),
            dma((4, max(n_seq, n_rep))),
            dma((4, max(n_seq, n_rep))),
            dma((2, n_rep)),
            dma((2, n_seq)),
            dma((2, n_seq)),
            dma((n_rep,)),
            dma((n_rep,)),
            dma((n_seq,)),
            dma((n_seq,)),
            dma((n_rep, n_seq)),
            dma((n_rep, n_seq)),
            dma((n_rep,)),
            dma((n_rep,)),
            dma((n_seq,)),
            dma((n_seq,)),
        ],
        compiler_params=pltpu.CompilerParams(
            collective_id=0, has_side_effects=True, vmem_limit_bytes=62 * 1024 * 1024
        ),
    )(
        block_order,
        queries,
        keys_new,
        values_new,
        keys_past,
        values_past,
        residual,
        norm_gain.reshape(1, -1),
        router.T,
        expert_ids.T,
        out_proj,
        w_gate,
        w_up,
        w_down,
    )
    return pl.pallas_call(
        hand_over,
        out_shape=tuple(jax.ShapeDtypeStruct(out.shape, out.dtype) for out in outs),
        in_specs=[vmem] * 4,
        out_specs=(vmem,) * 4,
    )(*outs)


def body(*arrays):
    queries, out_proj = arrays[0], arrays[7]
    n_seq, n_rep = lax.axis_size("seq"), lax.axis_size("rep")
    held = 2 * sum(math.prod(array.shape) for array in arrays[10:13])
    fits = held <= 50 * 1024 * 1024 and n_seq * STAT_ROWS <= 128 and n_seq == n_rep and n_rep % 2 == 0 and n_rep > 2
    if fits and out_proj.shape[0] == queries.shape[1]:
        return fused_body(*arrays)
    return plain_body(*arrays)


def solution(mesh):
    in_specs = (
        P(("groups", "seq"), "rep"),
        P(("groups", "seq"), "rep"),
        P(("groups", "seq"), "rep"),
        P(("groups", "seq"), "rep"),
        P(("groups", "seq"), "rep"),
        P("groups"),
        P(("groups", "seq"), "rep"),
        P("seq", "rep"),
        P(),
        P(),
        P("rep", None, "seq"),
        P("rep", None, "seq"),
        P("rep", "seq", None),
        P(("groups", "seq"), None),
    )
    out_specs = (
        P(("groups", "seq"), "rep"),
        P(("groups", "seq"), "rep"),
        P(("groups", "seq"), None),
        P(("groups", "seq"), None),
    )
    return jax.shard_map(body, mesh=mesh, in_specs=in_specs, out_specs=out_specs, check_vma=False)
```

profile of v0, /device:TPU:0, one launch (start us, length us, event | category | flops | bytes accessed | tf_op | source)
XLA Modules:
  0.0 53.9 jit_solution(935464253027734193)
XLA Ops:
  0.6 51.9 %shard_map.165 = (bf16[16,1024]{1,0:T(8,128)(2,1)}, bf16[16,1024]{1,0:T(8,128)(2,1)}, bf16[16,512]{1,0:T(8,128)(2,1)}, bf16[16,512]{1,0:T(8,128)(2,1)}) custom-call(s32[4]{0:T(128)} %order_ref.1, bf16[16,512]{1,0:T(8,128)(2,1)} %q_ref.1, bf16[16,128]{1,0:T(8,128)(2,1)} %kn_ref.1, bf16[16,128]{1,0:T(8,128)(2,1)} %vn_ref.1, bf16[256,128]{1,0:T(8,128)(2,1)} %kp_ref.1, ...), custom_call_target="tpu_custom_call" | custom-call | tf_op jit(solution)/shard_map/pallas_call | solution.py:664
  52.5 1.4 %shard_map.166 = (bf16[16,1024]{1,0:T(8,128)(2,1)}, bf16[16,1024]{1,0:T(8,128)(2,1)}, bf16[16,512]{1,0:T(8,128)(2,1)}, bf16[16,512]{1,0:T(8,128)(2,1)}) custom-call(bf16[16,1024]{1,0:T(8,128)(2,1)} %get-tuple-element.8.refs_0_, bf16[16,1024]{1,0:T(8,128)(2,1)} %get-tuple-element.9.refs_1_, bf16[16,512]{1,0:T(8,128)(2,1)} %get-tuple-element.10.refs_2_, ...), custom_call_target="tpu_custom_call" | custom-call | tf_op jit(solution)/shard_map/pallas_call | solution.py:735
where the time goes:
time: 54.2 us; the launch traced here: 53.9 us
  Pallas kernels  53.3 us (98%)
  between operations  0.64 us (1%)
    pallas_call x1, Pallas kernels, fused_body(): pl.pallas_call(functools.partial(fused_kernel, n_seq, n_rep), out_shape=(...  51.9 us
    pallas_call x1, Pallas kernels, fused_body(): pl.pallas_call(hand_over, out_shape=tuple((jax.ShapeDtypeStruct(out.shape...  1.42 us

commit v1 on v0

--- a/solution.py
+++ b/solution.py
@@ -140,6 +140,24 @@
 def fused_kernel(
     n_seq,
     n_rep,
+    order_hbm,
+    q_hbm,
+    kn_hbm,
+    vn_hbm,
+    kp_hbm,
+    vp_hbm,
+    res_hbm,
+    gain_hbm,
+    router_hbm,
+    ids_hbm,
+    proj_hbm,
+    gate_hbm,
+    up_hbm,
+    down_hbm,
+    att_out,
+    layer_out,
+    kc_out,
+    vc_out,
     order_ref,
     q_ref,
     kn_ref,
@@ -150,14 +168,7 @@
     gain_ref,
     router_ref,
     ids_ref,
-    proj_hbm,
-    gate_hbm,
-    up_hbm,
-    down_hbm,
-    att_out,
-    layer_out,
-    kc_out,
-    vc_out,
+    in_sem,
     wproj,
     wgate,
     wup,
@@ -237,6 +248,37 @@
     def rows_of(index):
         return pl.ds(pl.multiple_of(index * tok, tok), tok)
 
+    smalls = [
+        pltpu.make_async_copy(src, dst, in_sem.at[i])
+        for i, (src, dst) in enumerate(
+            (
+                (ids_hbm, ids_ref),
+                (q_hbm, q_ref),
+                (kn_hbm, kn_ref),
+                (vn_hbm, vn_ref),
+                (kp_hbm, kp_ref),
+                (vp_hbm, vp_ref),
+                (order_hbm, order_ref),
+                (res_hbm, res_ref),
+                (gain_hbm, gain_ref),
+                (router_hbm, router_ref),
+            )
+        )
+    ]
+    for small in smalls:
+        small.start()
+
+    barrier = pltpu.get_barrier_semaphore()
+    for i in reversed(range(n_seq)):
+        for j in reversed(range(n_rep)):
+            if i or j:
+                pl.semaphore_signal(
+                    barrier,
+                    inc=1,
+                    device_id=dev(other(seq, i, n_seq), other(rep, j, n_rep)),
+                    device_id_type=MESH,
+                )
+
     loads = []
     for i, (src, dst) in enumerate(
         ((proj_hbm, wproj), (gate_hbm.at[0], wgate), (up_hbm.at[0], wup), (down_hbm.at[0], wdown))
@@ -249,16 +291,8 @@
             load.start()
             loads.append(load)
 
-    barrier = pltpu.get_barrier_semaphore()
-    for i in range(n_seq):
-        for j in range(n_rep):
-            if i or j:
-                pl.semaphore_signal(
-                    barrier,
-                    inc=1,
-                    device_id=dev(other(seq, i, n_seq), other(rep, j, n_rep)),
-                    device_id_type=MESH,
-                )
+    for small in smalls[:4]:
+        small.wait()
     lane = lax.broadcasted_iota(jnp.int32, (tok, 128), 1)
     ids_f = ids_ref[...].astype(F32)
     diagonal = lax.broadcasted_iota(jnp.int32, (tok, tok), 0) == lax.broadcasted_iota(
@@ -296,6 +330,8 @@
             remote(idall.at[mine], idall.at[mine], small_send.at[1, k], small_recv.at[1, seq], to, rep)
         )
 
+    for small in smalls[4:]:
+        small.wait()
     own_pos = order_ref[seq] * tok + lax.broadcasted_iota(jnp.int32, (tok, tok), 1)
     bias = [
         jnp.where(
@@ -499,9 +535,8 @@
         )
 
     def add_quarter(at, start):
-        @pl.loop(0, hidden_width // chunk)
-        def _(c):
-            cols = pl.ds(pl.multiple_of(c * chunk, chunk), chunk)
+        for c in range(hidden_width // chunk):
+            cols = pl.ds(c * chunk, chunk)
             gate, up = products(at, cols)
             if start:
                 gate_acc[:, cols] = gate
@@ -533,9 +568,8 @@
     inverse = lax.rsqrt(squares / (feat * n_rep) + 1e-05)
     inverse_ref[...] = jnp.broadcast_to(inverse, (toks, 128))
 
-    @pl.loop(0, hidden_width // chunk)
-    def _(c):
-        cols = pl.ds(pl.multiple_of(c * chunk, chunk), chunk)
+    for c in range(hidden_width // chunk):
+        cols = pl.ds(c * chunk, chunk)
         factor = inverse_ref[:, 0:1]
         gate, up = products(last, cols)
         gate = (gate_acc[:, cols] + gate) * factor
@@ -629,8 +663,12 @@
 
 
 def hand_over(*refs):
-    for src, dst in zip(refs[:4], refs[4:]):
-        dst[...] = src[...]
+    sem = refs[8]
+    copies = [pltpu.make_async_copy(refs[i], refs[4 + i], sem.at[i]) for i in range(4)]
+    for copy in copies:
+        copy.start()
+    for copy in copies:
+        copy.wait()
 
 
 def fused_body(
@@ -657,21 +695,31 @@
     rows = toks * (width // hd)
     feat = residual.shape[1]
     vmem = pl.BlockSpec(memory_space=pltpu.VMEM)
-    smem = pl.BlockSpec(memory_space=pltpu.SMEM)
     hbm = pl.BlockSpec(memory_space=pl.ANY)
     dma = pltpu.SemaphoreType.DMA
     cache = (tok, hd * n_rep)
     outs = pl.pallas_call(
         functools.partial(fused_kernel, n_seq, n_rep),
         out_shape=(
-            jax.ShapeDtypeStruct((tok, feat), BF16),
-            jax.ShapeDtypeStruct((tok, feat), BF16),
-            jax.ShapeDtypeStruct(cache, BF16),
-            jax.ShapeDtypeStruct(cache, BF16),
+            pltpu.VMEM((tok, feat), BF16),
+            pltpu.VMEM((tok, feat), BF16),
+            pltpu.VMEM(cache, BF16),
+            pltpu.VMEM(cache, BF16),
         ),
-        in_specs=[smem] + [vmem] * 9 + [hbm] * 4,
+        in_specs=[hbm] * 14,
         out_specs=(vmem,) * 4,
         scratch_shapes=[
+            pltpu.SMEM(block_order.shape, jnp.int32),
+            pltpu.VMEM(queries.shape, BF16),
+            pltpu.VMEM(keys_new.shape, BF16),
+            pltpu.VMEM(values_new.shape, BF16),
+            pltpu.VMEM(keys_past.shape, BF16),
+            pltpu.VMEM(values_past.shape, BF16),
+            pltpu.VMEM(residual.shape, BF16),
+            pltpu.VMEM((1, norm_gain.shape[0]), F32),
+            pltpu.VMEM(router.shape[::-1], F32),
+            pltpu.VMEM(expert_ids.shape[::-1], jnp.int32),
+            dma((10,)),
             pltpu.VMEM(out_proj.shape, BF16),
             pltpu.VMEM(w_gate.shape[1:], BF16),
             pltpu.VMEM(w_up.shape[1:], BF16),
@@ -735,9 +783,10 @@
     return pl.pallas_call(
         hand_over,
         out_shape=tuple(jax.ShapeDtypeStruct(out.shape, out.dtype) for out in outs),
-        in_specs=[vmem] * 4,
-        out_specs=(vmem,) * 4,
-    )(*outs)
+        in_specs=[hbm] * 4,
+        out_specs=(hbm,) * 4,
+        scratch_shapes=[dma((4,))],
+    )(*[pltpu.with_memory_space_constraint(out, pltpu.VMEM) for out in outs])
 
 
 def body(*arrays):

time: 54.2 us -> 49.5 us (0.913)
  Pallas kernels: 53.3 us -> 48.7 us
    pallas_call x1, Pallas kernels: 51.9 us -> 48.1 us  [fused_body(): pl.pallas_call(functools.partial(fused_kernel, n_seq, n_rep), out_shape=(...]
    pallas_call x1, Pallas kernels: 1.42 us -> 0.67 us  [fused_body(): pl.pallas_call(hand_over, out_shape=tuple((jax.ShapeDtypeStruct(out.shape...]
where the time goes in v1:
time: 49.5 us; the launch traced here: 49.4 us
  Pallas kernels  48.7 us (98%)
  between operations  0.64 us (1%)
    pallas_call x1, Pallas kernels, fused_body(): pl.pallas_call(functools.partial(fused_kernel, n_seq, n_rep), out_shape=(...  48.1 us

profile of v1, /device:TPU:0, one launch (start us, length us, event | category | flops | bytes accessed | tf_op | source)
XLA Modules:
  0.0 49.4 jit_solution(17660362706897195138)
XLA Ops:
  0.6 48.1 %shard_map.165 = (bf16[16,1024]{1,0:T(8,128)(2,1)S(1)}, bf16[16,1024]{1,0:T(8,128)(2,1)S(1)}, bf16[16,512]{1,0:T(8,128)(2,1)S(1)}, bf16[16,512]{1,0:T(8,128)(2,1)S(1)}) custom-call(s32[4]{0:T(128)} %order_hbm.1, bf16[16,512]{1,0:T(8,128)(2,1)} %q_hbm.1, bf16[16,128]{1,0:T(8,128)(2,1)} %kn_hbm.1, bf16[16,128]{1,0:T(8,128)(2,1)} %vn_hbm.1, ...), custom_call_target="tpu_custom_call" | custom-call | tf_op jit(solution)/shard_map/pallas_call | solution.py:701
  48.7 0.7 %shard_map.166 = (bf16[16,1024]{1,0:T(8,128)(2,1)}, bf16[16,1024]{1,0:T(8,128)(2,1)}, bf16[16,512]{1,0:T(8,128)(2,1)}, bf16[16,512]{1,0:T(8,128)(2,1)}) custom-call(bf16[16,1024]{1,0:T(8,128)(2,1)S(1)} %get-tuple-element.8.refs_0_, bf16[16,1024]{1,0:T(8,128)(2,1)S(1)} %get-tuple-element.9.refs_1_, bf16[16,512]{1,0:T(8,128)(2,1)S(1)} %get-tuple-element.10.refs_2_, ...), custom_call_target="tpu_custom_call" | custom-call | tf_op jit(solution)/shard_map/pallas_call | solution.py:783

commit v2 on v1

v2 whole, which is shorter than its diff:
```python
import functools
import math

import jax
import jax.numpy as jnp
from jax import lax
from jax.experimental import pallas as pl
from jax.experimental.pallas import tpu as pltpu
from jax.sharding import PartitionSpec as P

EXPERTS = 4
CAP = 12


def block_lookup(owners, block_order):
    width = block_order.shape[0]
    hits = owners[:, None] == jnp.arange(width, dtype=jnp.int32)[None, :]
    return jnp.sum(jnp.where(hits, block_order[None, :], 0), axis=1)


def plain_body(
    queries,
    keys_new,
    values_new,
    keys_past,
    values_past,
    block_order,
    residual,
    out_proj,
    norm_gain,
    router,
    w_gate,
    w_up,
    w_down,
    expert_ids,
):
    seq_index = lax.axis_index("seq")
    rep_index = lax.axis_index("rep")
    rep_count = lax.axis_size("rep")
    tok_count = queries.shape[0]
    head_dim = keys_new.shape[1]
    q_per = queries.shape[1] // head_dim
    past_len = keys_past.shape[0]
    key_span = past_len + tok_count
    row_total = tok_count * q_per
    my_block = block_lookup(jnp.full((1,), seq_index, jnp.int32), block_order)[0]
    scaling = 1.0 / math.sqrt(head_dim)
    query_rows = queries.reshape(row_total, head_dim)
    query_pos = my_block * tok_count + jnp.arange(row_total, dtype=jnp.int32) // q_per
    keys_local = jnp.concatenate([keys_past, keys_new], axis=0)
    values_local = jnp.concatenate([values_past, values_new], axis=0)
    running = jnp.full((row_total,), -1e30, jnp.float32)
    key_piece = lax.all_gather(keys_local, "seq", axis=0, tiled=True)
    value_piece = lax.all_gather(values_local, "seq", axis=0, tiled=True)
    row_count = key_piece.shape[0]
    key_index = jnp.arange(row_count, dtype=jnp.int32)
    key_owner = key_index // key_span
    offset = key_index % key_span
    key_pos = block_lookup(key_owner, block_order) * tok_count + offset - past_len
    visible = (offset < past_len)[None, :] | (key_pos[None, :] <= query_pos[:, None])
    scores = jnp.dot(query_rows, key_piece.T, preferred_element_type=jnp.float32) * scaling
    highest = jnp.maximum(running, jnp.max(jnp.where(visible, scores, -1e30), axis=1))
    weights = jnp.where(visible, jnp.exp(scores - highest[:, None]), 0.0)
    totals = jnp.sum(weights, axis=1)
    numerator = jnp.dot(
        weights.astype(jnp.bfloat16), value_piece, preferred_element_type=jnp.float32
    )
    running, totals, numerator = (highest, totals, numerator)
    attn_local = (
        (numerator / totals[:, None]).reshape(tok_count, q_per * head_dim).astype(jnp.bfloat16)
    )
    attn_full, keys_cache, values_cache = (
        lax.all_gather(attn_local, "rep", axis=1, tiled=True),
        lax.all_gather(keys_new, "rep", axis=1, tiled=True),
        lax.all_gather(values_new, "rep", axis=1, tiled=True),
    )
    head_rows = lax.all_to_all(attn_full, "seq", split_axis=1, concat_axis=0, tiled=True)
    projected = lax.psum_scatter(
        jnp.dot(head_rows, out_proj, preferred_element_type=jnp.float32).astype(jnp.bfloat16),
        "seq",
        scatter_dimension=0,
        tiled=True,
    ).astype(jnp.float32)
    attended = (residual.astype(jnp.float32) + projected).astype(jnp.bfloat16)
    full_rows = lax.all_gather(attended, "rep", axis=1, tiled=True)
    features = full_rows.astype(jnp.float32)
    mean_square = jnp.mean(features * features, axis=1, keepdims=True)
    normed = (features * norm_gain[None, :] * lax.rsqrt(mean_square + 1e-05)).astype(jnp.bfloat16)
    logits = jnp.dot(normed.astype(jnp.float32), router, precision=lax.Precision.HIGHEST)
    expert_range = jnp.arange(EXPERTS, dtype=jnp.int32)
    first_pick = (expert_ids[:, 0:1] == expert_range[None, :]).astype(jnp.float32)
    second_pick = (expert_ids[:, 1:2] == expert_range[None, :]).astype(jnp.float32)
    share_first = jax.nn.sigmoid(
        jnp.sum(first_pick * logits, axis=1) - jnp.sum(second_pick * logits, axis=1)
    )
    token_share = share_first[:, None] * first_pick + (1.0 - share_first)[:, None] * second_pick
    member = first_pick + second_pick
    ranking = jnp.cumsum(member, axis=0) - member
    slot_range = jnp.arange(CAP, dtype=jnp.float32)
    selection = member.T[:, None, :] * (ranking.T[:, None, :] == slot_range[None, :, None]).astype(
        jnp.float32
    )
    mine_mask = (expert_range == rep_index % EXPERTS).astype(jnp.float32)
    my_selection = jnp.einsum("e,ejt->jt", mine_mask, selection)
    slot_rows = jnp.dot(
        my_selection.astype(jnp.bfloat16), normed, preferred_element_type=jnp.float32
    ).astype(jnp.bfloat16)
    gate_local = w_gate[0]
    up_local = w_up[0]
    down_local = w_down[0]
    piece = lax.all_gather(slot_rows, "seq", axis=0, tiled=True)
    gate_part = jnp.dot(piece, gate_local, preferred_element_type=jnp.float32)
    up_part = jnp.dot(piece, up_local, preferred_element_type=jnp.float32)
    hidden_slots = (jax.nn.silu(gate_part) * up_part).astype(jnp.bfloat16)
    expert_part = lax.psum_scatter(
        jnp.dot(hidden_slots, down_local, preferred_element_type=jnp.float32).astype(jnp.bfloat16),
        "seq",
        scatter_dimension=0,
        tiled=True,
    ).astype(jnp.float32)
    returned = lax.all_to_all(
        expert_part.astype(jnp.bfloat16), "rep", split_axis=1, concat_axis=0, tiled=True
    ).astype(expert_part.dtype)
    source_expert = jnp.arange(rep_count, dtype=jnp.int32) % EXPERTS
    source_pick = (source_expert[:, None] == expert_range[None, :]).astype(jnp.float32)
    combine = jnp.einsum("re,ejt,te->trj", source_pick, selection, token_share).reshape(
        tok_count, rep_count * CAP
    )
    moe_slice = jnp.dot(combine, returned, precision=lax.Precision.HIGHEST)
    layer_out = (attended.astype(jnp.float32) + moe_slice).astype(jnp.bfloat16)
    return (attended, layer_out, keys_cache, values_cache)


MESH = pl.DeviceIdType.MESH
HALF = 2
F32 = jnp.float32
BF16 = jnp.bfloat16


def fused_kernel(
    n_seq,
    n_rep,
    order_hbm,
    q_hbm,
    kn_hbm,
    vn_hbm,
    kp_hbm,
    vp_hbm,
    res_hbm,
    gain_hbm,
    router_hbm,
    ids_hbm,
    proj_hbm,
    gate_hbm,
    up_hbm,
    down_hbm,
    att_out,
    layer_out,
    kc_out,
    vc_out,
    order_ref,
    q_ref,
    kn_ref,
    vn_ref,
    kp_ref,
    vp_ref,
    res_ref,
    gain_ref,
    router_ref,
    ids_ref,
    in_sem,
    wproj,
    wgate,
    wup,
    wdown,
    qall,
    idall,
    kcache,
    vcache,
    num_send,
    num_all,
    head_send,
    head_all,
    res_all,
    part_send,
    part_all,
    xall,
    gained,
    router_split,
    gate_acc,
    up_acc,
    hidden,
    ysend,
    yall,
    psend,
    fin_all,
    w_sem,
    q_rsem,
    side_rsem,
    cache_rsem,
    cache_ssem,
    num_rsem,
    head_ssem,
    head_rsem,
    part_rsem,
    x_rsem,
    y_rsem,
    z_rsem,
    send_sem,
):
    group = lax.axis_index("groups")
    seq = lax.axis_index("seq")
    rep = lax.axis_index("rep")
    tok, width = q_ref.shape
    hd = kn_ref.shape[1]
    q_per = width // hd
    toks = tok * n_seq
    feat = res_ref.shape[1]
    slab = feat // n_seq
    stat_rows = num_send.shape[1] - tok * q_per

    chips = n_rep // 2
    chip, core = rep // 2, lax.rem(rep, 2)
    partner = chip * 2 + 1 - core

    def same_core(step):
        return lax.rem(chip + step, chips) * 2 + core

    def other_core(step):
        return lax.rem(chip + step, chips) * 2 + 1 - core

    def dev(s, r):
        return {"groups": group, "seq": s, "rep": r}

    def other(index, step, size):
        return lax.rem(index + step, size)

    def remote(src, dst, ssem, rsem, s, r):
        return pltpu.make_async_remote_copy(
            src_ref=src,
            dst_ref=dst,
            send_sem=ssem,
            recv_sem=rsem,
            device_id=dev(s, r),
            device_id_type=MESH,
        )

    def rows_of(index):
        return pl.ds(pl.multiple_of(index * tok, tok), tok)

    def split_terms(rest):
        terms = []
        for _ in range(3):
            terms.append(rest.astype(BF16).astype(F32))
            rest = rest - terms[-1]
        return terms

    def size_of(ref):
        return math.prod(ref.shape) * ref.dtype.itemsize

    def wait_all(sem, size):
        tiles = size // (16 * 128 * 2)
        wide = max(w for w in range(1, wgate.shape[1] // 128 + 1) if tiles % w == 0)
        span = wgate.at[pl.ds(0, tiles // wide * 16), pl.ds(0, wide * 128)]
        pltpu.make_async_copy(span, span, sem).wait()

    def slab_of(index):
        return pl.ds(pl.multiple_of(index * slab, slab), slab)

    def per_seq(rows):
        return [sum(jnp.where(seq == s, rows[s][k], 0) for s in range(n_seq)) for k in range(n_seq - 1)]

    def others(s):
        return [t for t in range(n_seq) if t != s]

    far_first = per_seq([sorted(others(s), key=lambda t: -abs(t - s)) for s in range(n_seq)])
    arrivals = per_seq(
        [
            sorted(others(s), key=lambda f: (abs(f - s), f if 2 * s < n_seq else -f))
            for s in range(n_seq)
        ]
    )

    smalls = [
        pltpu.make_async_copy(src, dst, in_sem.at[(0, 1, 2, 2, 3, 3, 4, 5, 6, 7)[i]])
        for i, (src, dst) in enumerate(
            (
                (ids_hbm, ids_ref),
                (q_hbm, q_ref),
                (kn_hbm, kn_ref),
                (vn_hbm, vn_ref),
                (kp_hbm, kp_ref),
                (vp_hbm, vp_ref),
                (order_hbm, order_ref),
                (res_hbm, res_ref),
                (gain_hbm, gain_ref),
                (router_hbm, router_ref),
            )
        )
    ]
    for small in smalls:
        small.start()

    barrier = pltpu.get_barrier_semaphore()
    for i in reversed(range(n_seq)):
        for j in reversed(range(n_rep)):
            if i or j:
                pl.semaphore_signal(
                    barrier,
                    inc=1,
                    device_id=dev(other(seq, i, n_seq), other(rep, j, n_rep)),
                    device_id_type=MESH,
                )

    loads = []
    for i, (src, dst) in enumerate(
        ((proj_hbm, wproj), (gate_hbm.at[0], wgate), (up_hbm.at[0], wup), (down_hbm.at[0], wdown))
    ):
        pieces = 1 if i == 0 else 4
        size = dst.shape[0] // pieces
        for j in range(pieces):
            span = pl.ds(j * size, size)
            pltpu.make_async_copy(src.at[span], dst.at[span], w_sem.at[i]).start()
        loads.append(pltpu.make_async_copy(src, dst, w_sem.at[i]))

    smalls[0].wait()
    smalls[1].wait()
    wait_all(in_sem.at[2], 2 * size_of(kn_ref))
    lane = lax.broadcasted_iota(jnp.int32, (tok, 128), 1)
    ids_f = ids_ref[...].astype(F32)
    diagonal = lax.broadcasted_iota(jnp.int32, (tok, tok), 0) == lax.broadcasted_iota(
        jnp.int32, (tok, tok), 1
    )
    picks = [
        jnp.sum(jnp.where(diagonal, ids_f[i : i + 1, :], 0.0), axis=1, keepdims=True)
        for i in range(2)
    ]
    idall[rows_of(seq), :] = jnp.where(lane == 0, picks[0], picks[1])
    qall[rows_of(seq), :] = q_ref[...]
    for j in range(n_rep):

        @pl.when(rep == j)
        def _():
            kcache[:, j * hd : (j + 1) * hd] = kn_ref[...]
            vcache[:, j * hd : (j + 1) * hd] = vn_ref[...]

    pl.semaphore_wait(barrier, n_seq * n_rep - 1)

    sent = [0]

    def send(ref, *rest):
        sent[0] += size_of(ref)
        remote(ref, rest[0], send_sem, *rest[1:]).start()

    mine = rows_of(seq)
    for to in far_first:
        send(q_ref, qall.at[mine], q_rsem, to, rep)

    experts = router_ref.shape[0]
    wait_all(in_sem.at[3], 2 * size_of(kp_ref))
    for small in smalls[6:]:
        small.wait()
    own_pos = order_ref[seq] * tok + lax.broadcasted_iota(jnp.int32, (tok, tok), 1)
    bias = [
        jnp.where(
            own_pos <= order_ref[t] * tok + lax.broadcasted_iota(jnp.int32, (tok, tok), 0),
            0.0,
            -1e30,
        )
        for t in range(n_seq)
    ]
    bias = jnp.concatenate([block for block in bias for _ in range(q_per)], axis=0)

    terms = split_terms(router_ref[...])
    terms.append(jnp.zeros((router_split.shape[0] - 3 * experts, router_ref.shape[1]), F32))
    router_split[...] = jnp.concatenate(terms, axis=0).astype(BF16)
    for to in far_first:
        send(res_ref.at[:, slab_of(to)], res_all.at[mine], side_rsem, to, rep)
        send(idall.at[mine], idall.at[mine], side_rsem, to, rep)
    res_all[mine, :] = res_ref[:, slab_of(seq)]

    wait_all(q_rsem, (n_seq - 1) * size_of(q_ref))

    scaling = 1.0 / math.sqrt(hd)
    queries = jnp.concatenate(
        [
            qall[t * tok : (t + 1) * tok, h * hd : (h + 1) * hd]
            for t in range(n_seq)
            for h in range(q_per)
        ],
        axis=0,
    )
    nt = (((1,), (1,)), ((), ()))
    s_past = lax.dot_general(queries, kp_ref[...], nt, preferred_element_type=F32) * scaling
    s_new = lax.dot_general(queries, kn_ref[...], nt, preferred_element_type=F32) * scaling + bias
    high = jnp.maximum(
        jnp.max(s_past, axis=1, keepdims=True), jnp.max(s_new, axis=1, keepdims=True)
    )
    w_past = jnp.exp(s_past - high)
    w_new = jnp.exp(s_new - high)
    total = jnp.sum(w_past, axis=1, keepdims=True) + jnp.sum(w_new, axis=1, keepdims=True)
    num = jnp.dot(w_past.astype(BF16), vp_ref[...], preferred_element_type=F32) + jnp.dot(
        w_new.astype(BF16), vn_ref[...], preferred_element_type=F32
    )
    rows = num.shape[0]
    stat_lane = lax.broadcasted_iota(jnp.int32, (rows, 128), 1)
    stats = jnp.where(stat_lane == 0, high, total).T
    span = rows // n_seq
    for t in range(n_seq):
        line = jnp.concatenate([stats[i : i + 1, t * span : (t + 1) * span] for i in range(2)], axis=1)
        coded = split_terms(line) + [jnp.zeros((stat_rows - 3, 2 * span), F32)]
        num_send[t, :span, :] = num[t * span : (t + 1) * span].astype(BF16)
        num_send[t, span:, :] = jnp.concatenate(coded, axis=0).astype(BF16)

    for to in far_first:
        send(num_send.at[to], num_all.at[seq], num_rsem, to, rep)
    num_all[seq] = num_send[seq]
    for j in range(n_rep):

        @pl.when(rep == j)
        def _():
            cols = pl.ds(j * hd, hd)
            for k in range(1, n_rep):
                to = (j + k) % n_rep
                remote(kn_ref, kcache.at[:, cols], cache_ssem, cache_rsem, seq, to).start()
                remote(vn_ref, vcache.at[:, cols], cache_ssem, cache_rsem, seq, to).start()

    wait_all(num_rsem, (n_seq - 1) * size_of(num_send.at[0]))

    lines = []
    for i in range(n_seq):
        coded = num_all[i, span:, :].astype(F32)
        lines.append(coded[0:1] + coded[1:2] + coded[2:3])
    lines.append(jnp.zeros((128 - n_seq, 2 * span), F32))
    stat_cols = jnp.concatenate(lines, axis=0).T
    highs = [stat_cols[:span, i : i + 1] for i in range(n_seq)]
    top = functools.reduce(jnp.maximum, highs)
    scales = [jnp.exp(h - top) for h in highs]
    full = sum(scales[i] * stat_cols[span:, i : i + 1] for i in range(n_seq))
    heads = sum(scales[i] * num_all[i, :span, :].astype(F32) for i in range(n_seq)) / full
    head_send[...] = heads.astype(BF16)

    def head_copy(to):
        return remote(head_send, head_all.at[seq], head_ssem, head_rsem, rep, to)

    for j in range(1, chips):
        send(head_send, head_all.at[seq], head_rsem, rep, same_core(j))
        send(head_send, head_all.at[seq], head_rsem, rep, other_core(j))

    @pl.when(seq != rep)
    def _():
        head_copy(rep).start()

    send(head_send, head_all.at[seq], head_rsem, rep, partner)

    @pl.when(seq == rep)
    def _():
        head_all[seq] = head_send[...]
        wait_all(head_rsem, (n_seq - 1) * size_of(head_send))

    @pl.when(seq != rep)
    def _():
        wait_all(head_rsem, n_seq * size_of(head_send))
        head_copy(rep).wait_send()

    head_rows = jnp.concatenate(
        [
            jnp.concatenate([head_all[t, h * tok : (h + 1) * tok, :] for t in range(n_seq)], axis=0)
            for h in range(q_per)
        ],
        axis=1,
    )
    loads[0].wait()
    wait_all(side_rsem, (n_seq - 1) * (tok * slab * 2 + tok * 128 * 4))
    for k, to in enumerate(far_first):
        part_send[k] = jnp.dot(
            head_rows, wproj[:, slab_of(to)], preferred_element_type=F32
        ).astype(BF16)
        send(part_send.at[k], part_all.at[seq], part_rsem, to, rep)
    summed = jnp.dot(head_rows, wproj[:, slab_of(seq)], preferred_element_type=F32)
    summed = summed.astype(BF16).astype(F32)
    wait_all(part_rsem, (n_seq - 1) * toks * slab * 2)
    for frm in arrivals:
        summed = summed + part_all[frm].astype(F32)
    xall[rep, seq] = (res_all[...].astype(F32) + summed).astype(BF16)

    def x_send(r, s, to_s, to_r):
        view = xall.at[r, s]
        send(view, view, x_rsem.at[r, s], to_s, to_r)

    def arrive(r, s):
        view = xall.at[r, s]
        remote(view, view, send_sem, x_rsem.at[r, s], seq, r).wait_recv()

    def spread(s, direct):
        for j in range(1, chips):
            x_send(rep, s, seq, same_core(j))
            if direct:
                x_send(rep, s, seq, other_core(j))
        x_send(rep, s, seq, partner)

    def from_seq(k):
        arrive(rep, arrivals[k])
        spread(arrivals[k], k > 0)

    def from_chip(s):
        for j in range(1, chips):
            arrive(same_core(j), s)
            x_send(same_core(j), s, seq, partner)

    spread(seq, False)
    for to in reversed(far_first):
        x_send(rep, seq, to, rep)
    hidden_width = wgate.shape[1]
    chunk = min(512, hidden_width)
    squares = [jnp.zeros((toks, 128), F32)]
    logits = [jnp.zeros((toks, router_split.shape[0]), F32)]

    def prepare(slots):
        for i, (r, s) in enumerate(slots):
            cols = pl.ds(pl.multiple_of(r * feat + s * slab, slab), slab)
            part = xall[r, s].astype(F32)
            squared = part * part
            for j in range(slab // 128):
                squares[0] = squares[0] + squared[:, j * 128 : (j + 1) * 128]
            scaled = (part * gain_ref[:, cols]).astype(BF16)
            gained[:, i * slab : (i + 1) * slab] = scaled
            logits[0] = logits[0] + lax.dot_general(
                scaled, router_split[:, cols], nt, preferred_element_type=F32
            )

    def products(slots, cols):
        total = None
        for i, (r, s) in enumerate(slots):
            span = pl.ds(pl.multiple_of(r * feat + s * slab, slab), slab)
            block = gained[:, i * slab : (i + 1) * slab]
            pair = (
                jnp.dot(block, wgate[span, cols], preferred_element_type=F32),
                jnp.dot(block, wup[span, cols], preferred_element_type=F32),
            )
            total = pair if total is None else (total[0] + pair[0], total[1] + pair[1])
        return total

    def add_slots(slots, start=False):
        prepare(slots)
        for c in range(hidden_width // chunk):
            cols = pl.ds(c * chunk, chunk)
            gate, up = products(slots, cols)
            if start:
                gate_acc[:, cols] = gate
                up_acc[:, cols] = up
            else:
                gate_acc[:, cols] += gate
                up_acc[:, cols] += up

    for load in loads[1:3]:
        load.wait()
    arrive(partner, seq)
    add_slots([(rep, seq), (partner, seq)], True)
    from_seq(0)
    from_chip(seq)
    add_slots([(rep, arrivals[0]), (same_core(1), seq)])
    for k in range(1, n_seq - 1):
        from_seq(k)
    att_out[...] = jnp.concatenate([xall[rep, t, mine] for t in range(n_seq)], axis=1)
    arrive(partner, arrivals[0])
    arrive(other_core(1), seq)
    add_slots([(partner, arrivals[0]), (other_core(1), seq)])
    from_chip(arrivals[0])
    rest = arrivals[1:]
    add_slots([(rep, s) for s in rest])
    for s in rest:
        arrive(partner, s)
    add_slots([(partner, s) for s in rest])
    for s in rest[:-1]:
        arrive(same_core(1), s)
    add_slots([(same_core(1), s) for s in arrivals[:-1]])
    for s in arrivals[:-1]:
        arrive(other_core(1), s)
    add_slots([(other_core(1), s) for s in arrivals[:-1]])
    final = [(same_core(1), arrivals[-1]), (other_core(1), arrivals[-1])]
    for slot in final:
        arrive(*slot)
    prepare(final)
    square = jnp.sum(squares[0], axis=1, keepdims=True)
    inverse = lax.rsqrt(square / (feat * n_rep) + 1e-05)
    for c in range(hidden_width // chunk):
        cols = pl.ds(c * chunk, chunk)
        gate, up = products(final, cols)
        gate = (gate_acc[:, cols] + gate) * inverse
        up = (up_acc[:, cols] + up) * inverse
        hidden[:, cols] = (gate * jax.nn.sigmoid(gate) * up).astype(BF16)

    columns = [
        sum(logits[0][:, i * experts + e : i * experts + e + 1] for i in range(3)) * inverse
        for e in range(experts)
    ]
    first = [(idall[:, 0:1] == float(e)).astype(F32) for e in range(experts)]
    second = [(idall[:, 1:2] == float(e)).astype(F32) for e in range(experts)]
    gap = sum(first[e] * columns[e] for e in range(experts)) - sum(
        second[e] * columns[e] for e in range(experts)
    )
    share = jax.nn.sigmoid(gap)
    mine_first = (idall[:, 0:1] == (rep % experts).astype(F32)).astype(F32)
    mine_second = (idall[:, 1:2] == (rep % experts).astype(F32)).astype(F32)
    weight = share * mine_first + (1.0 - share) * mine_second

    loads[3].wait()
    half = feat // HALF

    def weighted(to_chip, to_core, h):
        start = (to_chip * 2 + to_core) * feat + h * half
        cols = pl.ds(pl.multiple_of(start, half), half)
        product = jnp.dot(hidden[...], wdown[:, cols], preferred_element_type=F32)
        return product * weight

    def y_wait(j, h):
        remote(ysend.at[j, h], yall.at[j, h], send_sem, y_rsem.at[j, h], seq, partner).wait_recv()

    def to_partner(j, h, product):
        ysend[j, h] = product.astype(BF16)
        send(ysend.at[j, h], yall.at[j, h], y_rsem.at[j, h], seq, partner)

    def to_owner(j, h, product):
        y_wait(j, h)
        psend[j, h] = (product + yall[j, h].astype(F32)).astype(BF16)
        owner = lax.rem(chip + j, chips) * 2 + core
        for to in far_first + [seq] * min(j, 1):
            place = fin_all.at[seq, chip, :, pl.ds(h * half, half)]
            send(psend.at[j, h, rows_of(to)], place, z_rsem.at[seq, chip], to, owner)

    far = range(1, chips)
    steps = [(j, h, True) for j in far for h in range(HALF)] + [(0, 0, True)]
    steps += [(j, h, False) for j in far for h in range(HALF)]
    steps += [(0, h, True) for h in range(1, HALF)] + [(0, h, False) for h in range(HALF)]
    held = None
    for j, h, cross in steps:
        product = weighted(lax.rem(chip + j, chips), 1 - core if cross else core, h)
        if held is not None:
            held()
        held = functools.partial(to_partner if cross else to_owner, j, h, product)
    held()

    wait_all(cache_rsem, 2 * (n_rep - 1) * size_of(kn_ref))
    kc_out[...] = kcache[...]
    vc_out[...] = vcache[...]
    wait_all(cache_ssem, 2 * (n_rep - 1) * size_of(kn_ref))
    wait_all(send_sem, sent[0])

    own = jnp.concatenate([psend[0, h, mine] for h in range(HALF)], axis=1)
    result = att_out[...].astype(F32) + own.astype(F32)
    for frm_s, frm_chip in [(seq, lax.rem(chip + j, chips)) for j in range(1, chips)] + [
        (s, lax.rem(chip + j, chips)) for s in arrivals for j in range(chips)
    ]:
        place = fin_all.at[frm_s, frm_chip]
        remote(place, place, send_sem, z_rsem.at[frm_s, frm_chip], frm_s, rep).wait_recv()
        result = result + fin_all[frm_s, frm_chip].astype(F32)
    layer_out[...] = result.astype(BF16)


def hand_over(*refs):
    sem = refs[8]
    copies = [pltpu.make_async_copy(refs[i], refs[4 + i], sem.at[i]) for i in range(4)]
    for copy in copies:
        copy.start()
    for copy in copies:
        copy.wait()


def fused_body(
    queries,
    keys_new,
    values_new,
    keys_past,
    values_past,
    block_order,
    residual,
    out_proj,
    norm_gain,
    router,
    w_gate,
    w_up,
    w_down,
    expert_ids,
):
    n_seq = lax.axis_size("seq")
    n_rep = lax.axis_size("rep")
    tok, width = queries.shape
    hd = keys_new.shape[1]
    toks = tok * n_seq
    rows = toks * (width // hd)
    feat = residual.shape[1]
    slab = feat // n_seq
    chips = n_rep // 2
    vmem = pl.BlockSpec(memory_space=pltpu.VMEM)
    hbm = pl.BlockSpec(memory_space=pl.ANY)
    dma = pltpu.SemaphoreType.DMA
    cache = (tok, hd * n_rep)
    outs = pl.pallas_call(
        functools.partial(fused_kernel, n_seq, n_rep),
        out_shape=(
            pltpu.VMEM((tok, feat), BF16),
            pltpu.VMEM((tok, feat), BF16),
            pltpu.VMEM(cache, BF16),
            pltpu.VMEM(cache, BF16),
        ),
        in_specs=[hbm] * 14,
        out_specs=(vmem,) * 4,
        scratch_shapes=[
            pltpu.SMEM(block_order.shape, jnp.int32),
            pltpu.VMEM(queries.shape, BF16),
            pltpu.VMEM(keys_new.shape, BF16),
            pltpu.VMEM(values_new.shape, BF16),
            pltpu.VMEM(keys_past.shape, BF16),
            pltpu.VMEM(values_past.shape, BF16),
            pltpu.VMEM(residual.shape, BF16),
            pltpu.VMEM((1, norm_gain.shape[0]), F32),
            pltpu.VMEM(router.shape[::-1], F32),
            pltpu.VMEM(expert_ids.shape[::-1], jnp.int32),
            dma((9,)),
            pltpu.VMEM(out_proj.shape, BF16),
            pltpu.VMEM(w_gate.shape[1:], BF16),
            pltpu.VMEM(w_up.shape[1:], BF16),
            pltpu.VMEM(w_down.shape[1:], BF16),
            pltpu.VMEM((toks, width), BF16),
            pltpu.VMEM((toks, 128), F32),
            pltpu.VMEM(cache, BF16),
            pltpu.VMEM(cache, BF16),
            pltpu.VMEM((n_seq, rows // n_seq + 16, hd), BF16),
            pltpu.VMEM((n_seq, rows // n_seq + 16, hd), BF16),
            pltpu.VMEM((rows // n_seq, hd), BF16),
            pltpu.VMEM((n_seq, rows // n_seq, hd), BF16),
            pltpu.VMEM((toks, slab), BF16),
            pltpu.VMEM((n_seq - 1, toks, slab), BF16),
            pltpu.VMEM((n_seq, toks, slab), BF16),
            pltpu.VMEM((n_rep, n_seq, toks, slab), BF16),
            pltpu.VMEM((toks, (n_seq - 2) * slab), BF16),
            pltpu.VMEM((16, norm_gain.shape[0]), BF16),
            pltpu.VMEM((toks, w_gate.shape[2]), F32),
            pltpu.VMEM((toks, w_gate.shape[2]), F32),
            pltpu.VMEM((toks, w_gate.shape[2]), BF16),
            pltpu.VMEM((chips, HALF, toks, feat // HALF), BF16),
            pltpu.VMEM((chips, HALF, toks, feat // HALF), BF16),
            pltpu.VMEM((chips, HALF, toks, feat // HALF), BF16),
            pltpu.VMEM((n_seq, chips, tok, feat), BF16),
            dma((4,)),
            dma,
            dma,
            dma,
            dma,
            dma,
            dma,
            dma,
            dma,
            dma((n_rep, n_seq)),
            dma((chips, HALF)),
            dma((n_seq, chips)),
            dma,
        ],
        compiler_params=pltpu.CompilerParams(
            collective_id=0, has_side_effects=True, vmem_limit_bytes=62 * 1024 * 1024
        ),
    )(
        block_order,
        queries,
        keys_new,
        values_new,
        keys_past,
        values_past,
        residual,
        norm_gain.reshape(1, -1),
        router.T,
        expert_ids.T,
        out_proj,
        w_gate,
        w_up,
        w_down,
    )
    return pl.pallas_call(
        hand_over,
        out_shape=tuple(jax.ShapeDtypeStruct(out.shape, out.dtype) for out in outs),
        in_specs=[hbm] * 4,
        out_specs=(hbm,) * 4,
        scratch_shapes=[dma((4,))],
    )(*[pltpu.with_memory_space_constraint(out, pltpu.VMEM) for out in outs])


def body(*arrays):
    queries, out_proj = arrays[0], arrays[7]
    n_seq, n_rep = lax.axis_size("seq"), lax.axis_size("rep")
    held = 2 * sum(math.prod(array.shape) for array in arrays[10:13])
    tok, width, hd = queries.shape[0], queries.shape[1], arrays[1].shape[1]
    fits = held <= 50 * 1024 * 1024 and n_seq == n_rep and n_rep == 4
    fits = fits and 2 * tok * (width // hd) == hd == 128 and tok % 16 == 0
    if fits and out_proj.shape[0] == queries.shape[1]:
        return fused_body(*arrays)
    return plain_body(*arrays)


def solution(mesh):
    in_specs = (
        P(("groups", "seq"), "rep"),
        P(("groups", "seq"), "rep"),
        P(("groups", "seq"), "rep"),
        P(("groups", "seq"), "rep"),
        P(("groups", "seq"), "rep"),
        P("groups"),
        P(("groups", "seq"), "rep"),
        P("seq", "rep"),
        P(),
        P(),
        P("rep", None, "seq"),
        P("rep", None, "seq"),
        P("rep", "seq", None),
        P(("groups", "seq"), None),
    )
    out_specs = (
        P(("groups", "seq"), "rep"),
        P(("groups", "seq"), "rep"),
        P(("groups", "seq"), None),
        P(("groups", "seq"), None),
    )
    return jax.shard_map(body, mesh=mesh, in_specs=in_specs, out_specs=out_specs, check_vma=False)
```

time: 49.5 us -> 44.4 us (0.90)
  Pallas kernels: 48.7 us -> 43.6 us
    pallas_call x1, Pallas kernels: 48.1 us -> 43 us  [fused_body(): pl.pallas_call(functools.partial(fused_kernel, n_seq, n_rep), out_shape=(...]
where the time goes in v2:
time: 44.4 us; the launch traced here: 44.3 us
  Pallas kernels  43.6 us (98%)
  between operations  0.64 us (1%)
    pallas_call x1, Pallas kernels, fused_body(): pl.pallas_call(functools.partial(fused_kernel, n_seq, n_rep), out_shape=(...  43 us

profile of v2, /device:TPU:0, one launch (start us, length us, event | category | flops | bytes accessed | tf_op | source)
XLA Modules:
  0.0 44.3 jit_solution(6047792976476080184)
XLA Ops:
  0.6 43.0 %shard_map.165 = (bf16[16,1024]{1,0:T(8,128)(2,1)S(1)}, bf16[16,1024]{1,0:T(8,128)(2,1)S(1)}, bf16[16,512]{1,0:T(8,128)(2,1)S(1)}, bf16[16,512]{1,0:T(8,128)(2,1)S(1)}) custom-call(s32[4]{0:T(128)} %order_hbm.1, bf16[16,512]{1,0:T(8,128)(2,1)} %q_hbm.1, bf16[16,128]{1,0:T(8,128)(2,1)} %kn_hbm.1, bf16[16,128]{1,0:T(8,128)(2,1)} %vn_hbm.1, ...), custom_call_target="tpu_custom_call" | custom-call | tf_op jit(solution)/shard_map/pallas_call | solution.py:699
  43.6 0.7 %shard_map.166 = (bf16[16,1024]{1,0:T(8,128)(2,1)}, bf16[16,1024]{1,0:T(8,128)(2,1)}, bf16[16,512]{1,0:T(8,128)(2,1)}, bf16[16,512]{1,0:T(8,128)(2,1)}) custom-call(bf16[16,1024]{1,0:T(8,128)(2,1)S(1)} %get-tuple-element.8.refs_0_, bf16[16,1024]{1,0:T(8,128)(2,1)S(1)} %get-tuple-element.9.refs_1_, bf16[16,512]{1,0:T(8,128)(2,1)S(1)} %get-tuple-element.10.refs_2_, ...), custom_call_target="tpu_custom_call" | custom-call | tf_op jit(solution)/shard_map/pallas_call | solution.py:779

commit v3 on v2

--- a/solution.py
+++ b/solution.py
@@ -354,23 +354,13 @@
 
     mine = rows_of(seq)
     for to in far_first:
-        send(q_ref, qall.at[mine], q_rsem, to, rep)
+        send(q_ref, qall.at[mine], q_rsem.at[seq], to, rep)
 
     experts = router_ref.shape[0]
     wait_all(in_sem.at[3], 2 * size_of(kp_ref))
     for small in smalls[6:]:
         small.wait()
     own_pos = order_ref[seq] * tok + lax.broadcasted_iota(jnp.int32, (tok, tok), 1)
-    bias = [
-        jnp.where(
-            own_pos <= order_ref[t] * tok + lax.broadcasted_iota(jnp.int32, (tok, tok), 0),
-            0.0,
-            -1e30,
-        )
-        for t in range(n_seq)
-    ]
-    bias = jnp.concatenate([block for block in bias for _ in range(q_per)], axis=0)
-
     terms = split_terms(router_ref[...])
     terms.append(jnp.zeros((router_split.shape[0] - 3 * experts, router_ref.shape[1]), F32))
     router_split[...] = jnp.concatenate(terms, axis=0).astype(BF16)
@@ -378,43 +368,6 @@
         send(res_ref.at[:, slab_of(to)], res_all.at[mine], side_rsem, to, rep)
         send(idall.at[mine], idall.at[mine], side_rsem, to, rep)
     res_all[mine, :] = res_ref[:, slab_of(seq)]
-
-    wait_all(q_rsem, (n_seq - 1) * size_of(q_ref))
-
-    scaling = 1.0 / math.sqrt(hd)
-    queries = jnp.concatenate(
-        [
-            qall[t * tok : (t + 1) * tok, h * hd : (h + 1) * hd]
-            for t in range(n_seq)
-            for h in range(q_per)
-        ],
-        axis=0,
-    )
-    nt = (((1,), (1,)), ((), ()))
-    s_past = lax.dot_general(queries, kp_ref[...], nt, preferred_element_type=F32) * scaling
-    s_new = lax.dot_general(queries, kn_ref[...], nt, preferred_element_type=F32) * scaling + bias
-    high = jnp.maximum(
-        jnp.max(s_past, axis=1, keepdims=True), jnp.max(s_new, axis=1, keepdims=True)
-    )
-    w_past = jnp.exp(s_past - high)
-    w_new = jnp.exp(s_new - high)
-    total = jnp.sum(w_past, axis=1, keepdims=True) + jnp.sum(w_new, axis=1, keepdims=True)
-    num = jnp.dot(w_past.astype(BF16), vp_ref[...], preferred_element_type=F32) + jnp.dot(
-        w_new.astype(BF16), vn_ref[...], preferred_element_type=F32
-    )
-    rows = num.shape[0]
-    stat_lane = lax.broadcasted_iota(jnp.int32, (rows, 128), 1)
-    stats = jnp.where(stat_lane == 0, high, total).T
-    span = rows // n_seq
-    for t in range(n_seq):
-        line = jnp.concatenate([stats[i : i + 1, t * span : (t + 1) * span] for i in range(2)], axis=1)
-        coded = split_terms(line) + [jnp.zeros((stat_rows - 3, 2 * span), F32)]
-        num_send[t, :span, :] = num[t * span : (t + 1) * span].astype(BF16)
-        num_send[t, span:, :] = jnp.concatenate(coded, axis=0).astype(BF16)
-
-    for to in far_first:
-        send(num_send.at[to], num_all.at[seq], num_rsem, to, rep)
-    num_all[seq] = num_send[seq]
     for j in range(n_rep):
 
         @pl.when(rep == j)
@@ -424,6 +377,41 @@
                 to = (j + k) % n_rep
                 remote(kn_ref, kcache.at[:, cols], cache_ssem, cache_rsem, seq, to).start()
                 remote(vn_ref, vcache.at[:, cols], cache_ssem, cache_rsem, seq, to).start()
+
+    scaling = 1.0 / math.sqrt(hd)
+    nt = (((1,), (1,)), ((), ()))
+    span = tok * q_per
+    row = lax.broadcasted_iota(jnp.int32, (tok, tok), 0)
+
+    def attend(t, out):
+        block = qall[rows_of(t), :]
+        block = jnp.concatenate([block[:, h * hd : (h + 1) * hd] for h in range(q_per)], axis=0)
+        bias = jnp.where(own_pos <= order_ref[t] * tok + row, 0.0, -1e30)
+        bias = jnp.concatenate([bias] * q_per, axis=0)
+        s_past = lax.dot_general(block, kp_ref[...], nt, preferred_element_type=F32) * scaling
+        s_new = lax.dot_general(block, kn_ref[...], nt, preferred_element_type=F32) * scaling + bias
+        high = jnp.maximum(
+            jnp.max(s_past, axis=1, keepdims=True), jnp.max(s_new, axis=1, keepdims=True)
+        )
+        w_past = jnp.exp(s_past - high)
+        w_new = jnp.exp(s_new - high)
+        total = jnp.sum(w_past, axis=1, keepdims=True) + jnp.sum(w_new, axis=1, keepdims=True)
+        num = jnp.dot(w_past.astype(BF16), vp_ref[...], preferred_element_type=F32) + jnp.dot(
+            w_new.astype(BF16), vn_ref[...], preferred_element_type=F32
+        )
+        stat_lane = lax.broadcasted_iota(jnp.int32, (span, 128), 1)
+        stats = jnp.where(stat_lane == 0, high, total).T
+        line = jnp.concatenate([stats[i : i + 1, :] for i in range(2)], axis=1)
+        coded = split_terms(line) + [jnp.zeros((stat_rows - 3, 2 * span), F32)]
+        out[:span, :] = num.astype(BF16)
+        out[span:, :] = jnp.concatenate(coded, axis=0).astype(BF16)
+
+    attend(seq, num_all.at[seq])
+    for frm in arrivals:
+        src = rows_of(frm)
+        remote(q_ref, qall.at[src], send_sem, q_rsem.at[frm], frm, rep).wait_recv()
+        attend(frm, num_send.at[frm])
+        send(num_send.at[frm], num_all.at[seq], num_rsem, frm, rep)
 
     wait_all(num_rsem, (n_seq - 1) * size_of(num_send.at[0]))
 
@@ -441,47 +429,54 @@
     head_send[...] = heads.astype(BF16)
 
     def head_copy(to):
-        return remote(head_send, head_all.at[seq], head_ssem, head_rsem, rep, to)
+        return remote(head_send, head_all.at[seq], head_ssem, head_rsem.at[seq], rep, to)
 
     for j in range(1, chips):
-        send(head_send, head_all.at[seq], head_rsem, rep, same_core(j))
-        send(head_send, head_all.at[seq], head_rsem, rep, other_core(j))
+        send(head_send, head_all.at[seq], head_rsem.at[seq], rep, same_core(j))
+        send(head_send, head_all.at[seq], head_rsem.at[seq], rep, other_core(j))
 
     @pl.when(seq != rep)
     def _():
         head_copy(rep).start()
 
-    send(head_send, head_all.at[seq], head_rsem, rep, partner)
+    send(head_send, head_all.at[seq], head_rsem.at[seq], rep, partner)
+    loads[0].wait()
+
+    def head_wait(f):
+        remote(head_send, head_all.at[f], head_ssem, head_rsem.at[f], seq, rep).wait_recv()
+
+    def project(f):
+        block = jnp.concatenate(
+            [head_all[f, h * tok : (h + 1) * tok, :] for h in range(q_per)], axis=1
+        )
+        part = jnp.dot(block, wproj[...], preferred_element_type=F32).astype(BF16)
+        for t in range(n_seq):
+            part_send[f, t] = part[:, t * slab : (t + 1) * slab]
+        for to in far_first:
+            send(part_send.at[f, to], part_all.at[seq, rows_of(f)], part_rsem, to, rep)
+        part_all[seq, rows_of(f), :] = part_send[f, seq]
 
     @pl.when(seq == rep)
     def _():
         head_all[seq] = head_send[...]
-        wait_all(head_rsem, (n_seq - 1) * size_of(head_send))
 
     @pl.when(seq != rep)
     def _():
-        wait_all(head_rsem, n_seq * size_of(head_send))
+        head_wait(seq)
+
+    project(seq)
+    for f in arrivals:
+        head_wait(f)
+        project(f)
+
+    wait_all(side_rsem, (n_seq - 1) * (tok * slab * 2 + tok * 128 * 4))
+
+    @pl.when(seq != rep)
+    def _():
         head_copy(rep).wait_send()
 
-    head_rows = jnp.concatenate(
-        [
-            jnp.concatenate([head_all[t, h * tok : (h + 1) * tok, :] for t in range(n_seq)], axis=0)
-            for h in range(q_per)
-        ],
-        axis=1,
-    )
-    loads[0].wait()
-    wait_all(side_rsem, (n_seq - 1) * (tok * slab * 2 + tok * 128 * 4))
-    for k, to in enumerate(far_first):
-        part_send[k] = jnp.dot(
-            head_rows, wproj[:, slab_of(to)], preferred_element_type=F32
-        ).astype(BF16)
-        send(part_send.at[k], part_all.at[seq], part_rsem, to, rep)
-    summed = jnp.dot(head_rows, wproj[:, slab_of(seq)], preferred_element_type=F32)
-    summed = summed.astype(BF16).astype(F32)
     wait_all(part_rsem, (n_seq - 1) * toks * slab * 2)
-    for frm in arrivals:
-        summed = summed + part_all[frm].astype(F32)
+    summed = sum(part_all[f].astype(F32) for f in range(n_seq))
     xall[rep, seq] = (res_all[...].astype(F32) + summed).astype(BF16)
 
     def x_send(r, s, to_s, to_r):
@@ -559,16 +554,17 @@
     add_slots([(rep, seq), (partner, seq)], True)
     from_seq(0)
     from_chip(seq)
+    from_seq(1)
     add_slots([(rep, arrivals[0]), (same_core(1), seq)])
-    for k in range(1, n_seq - 1):
+    for k in range(2, n_seq - 1):
         from_seq(k)
     att_out[...] = jnp.concatenate([xall[rep, t, mine] for t in range(n_seq)], axis=1)
     arrive(partner, arrivals[0])
     arrive(other_core(1), seq)
     add_slots([(partner, arrivals[0]), (other_core(1), seq)])
-    from_chip(arrivals[0])
     rest = arrivals[1:]
     add_slots([(rep, s) for s in rest])
+    from_chip(arrivals[0])
     for s in rest:
         arrive(partner, s)
     add_slots([(partner, s) for s in rest])
@@ -578,6 +574,7 @@
     for s in arrivals[:-1]:
         arrive(other_core(1), s)
     add_slots([(other_core(1), s) for s in arrivals[:-1]])
+    loads[3].wait()
     final = [(same_core(1), arrivals[-1]), (other_core(1), arrivals[-1])]
     for slot in final:
         arrive(*slot)
@@ -605,41 +602,37 @@
     mine_second = (idall[:, 1:2] == (rep % experts).astype(F32)).astype(F32)
     weight = share * mine_first + (1.0 - share) * mine_second
 
-    loads[3].wait()
-    half = feat // HALF
-
-    def weighted(to_chip, to_core, h):
-        start = (to_chip * 2 + to_core) * feat + h * half
-        cols = pl.ds(pl.multiple_of(start, half), half)
-        product = jnp.dot(hidden[...], wdown[:, cols], preferred_element_type=F32)
-        return product * weight
-
-    def y_wait(j, h):
-        remote(ysend.at[j, h], yall.at[j, h], send_sem, y_rsem.at[j, h], seq, partner).wait_recv()
-
-    def to_partner(j, h, product):
-        ysend[j, h] = product.astype(BF16)
-        send(ysend.at[j, h], yall.at[j, h], y_rsem.at[j, h], seq, partner)
-
-    def to_owner(j, h, product):
-        y_wait(j, h)
-        psend[j, h] = (product + yall[j, h].astype(F32)).astype(BF16)
+    def weighted(to_chip, to_core, at, size):
+        start = (to_chip * 2 + to_core) * feat + at
+        cols = pl.ds(pl.multiple_of(start, size), size)
+        return jnp.dot(hidden[...], wdown[:, cols], preferred_element_type=F32) * weight
+
+    def cross(j, h, parts):
+        size = feat // parts
+        cols = pl.ds(h * size, size)
+        ysend[j, :, cols] = weighted(lax.rem(chip + j, chips), 1 - core, h * size, size).astype(BF16)
+        send(ysend.at[j, :, cols], yall.at[j, :, cols], y_rsem.at[j, h], seq, partner)
+
+    def keep(j, h, parts):
+        size = feat // parts
+        cols = pl.ds(h * size, size)
+        product = weighted(lax.rem(chip + j, chips), core, h * size, size)
+        view = yall.at[j, :, cols]
+        remote(view, view, send_sem, y_rsem.at[j, h], seq, partner).wait_recv()
+        psend[j, :, cols] = (product + yall[j, :, cols].astype(F32)).astype(BF16)
         owner = lax.rem(chip + j, chips) * 2 + core
         for to in far_first + [seq] * min(j, 1):
-            place = fin_all.at[seq, chip, :, pl.ds(h * half, half)]
-            send(psend.at[j, h, rows_of(to)], place, z_rsem.at[seq, chip], to, owner)
-
-    far = range(1, chips)
-    steps = [(j, h, True) for j in far for h in range(HALF)] + [(0, 0, True)]
-    steps += [(j, h, False) for j in far for h in range(HALF)]
-    steps += [(0, h, True) for h in range(1, HALF)] + [(0, h, False) for h in range(HALF)]
-    held = None
-    for j, h, cross in steps:
-        product = weighted(lax.rem(chip + j, chips), 1 - core if cross else core, h)
-        if held is not None:
-            held()
-        held = functools.partial(to_partner if cross else to_owner, j, h, product)
-    held()
+            place = fin_all.at[seq, chip, :, cols]
+            send(psend.at[j, rows_of(to), cols], place, z_rsem.at[seq, chip], to, owner)
+
+    for j in range(1, chips):
+        for h in range(HALF):
+            cross(j, h, HALF)
+    for j in range(1, chips):
+        for h in range(HALF):
+            keep(j, h, HALF)
+    cross(0, 0, 1)
+    keep(0, 0, 1)
 
     wait_all(cache_rsem, 2 * (n_rep - 1) * size_of(kn_ref))
     kc_out[...] = kcache[...]
@@ -647,8 +640,7 @@
     wait_all(cache_ssem, 2 * (n_rep - 1) * size_of(kn_ref))
     wait_all(send_sem, sent[0])
 
-    own = jnp.concatenate([psend[0, h, mine] for h in range(HALF)], axis=1)
-    result = att_out[...].astype(F32) + own.astype(F32)
+    result = att_out[...].astype(F32) + psend[0, mine, :].astype(F32)
     for frm_s, frm_chip in [(seq, lax.rem(chip + j, chips)) for j in range(1, chips)] + [
         (s, lax.rem(chip + j, chips)) for s in arrivals for j in range(chips)
     ]:
@@ -731,7 +723,7 @@
             pltpu.VMEM((rows // n_seq, hd), BF16),
             pltpu.VMEM((n_seq, rows // n_seq, hd), BF16),
             pltpu.VMEM((toks, slab), BF16),
-            pltpu.VMEM((n_seq - 1, toks, slab), BF16),
+            pltpu.VMEM((n_seq, n_seq, tok, slab), BF16),
             pltpu.VMEM((n_seq, toks, slab), BF16),
             pltpu.VMEM((n_rep, n_seq, toks, slab), BF16),
             pltpu.VMEM((toks, (n_seq - 2) * slab), BF16),
@@ -739,18 +731,18 @@
             pltpu.VMEM((toks, w_gate.shape[2]), F32),
             pltpu.VMEM((toks, w_gate.shape[2]), F32),
             pltpu.VMEM((toks, w_gate.shape[2]), BF16),
-            pltpu.VMEM((chips, HALF, toks, feat // HALF), BF16),
-            pltpu.VMEM((chips, HALF, toks, feat // HALF), BF16),
-            pltpu.VMEM((chips, HALF, toks, feat // HALF), BF16),
+            pltpu.VMEM((chips, toks, feat), BF16),
+            pltpu.VMEM((chips, toks, feat), BF16),
+            pltpu.VMEM((chips, toks, feat), BF16),
             pltpu.VMEM((n_seq, chips, tok, feat), BF16),
             dma((4,)),
+            dma((n_seq,)),
             dma,
             dma,
             dma,
             dma,
             dma,
-            dma,
-            dma,
+            dma((n_seq,)),
             dma,
             dma((n_rep, n_seq)),
             dma((chips, HALF)),

time: 44.4 us -> 42.2 us (0.950)
  Pallas kernels: 43.6 us -> 41.3 us
    pallas_call x1, Pallas kernels: 43 us -> 40.7 us  [fused_body(): pl.pallas_call(functools.partial(fused_kernel, n_seq, n_rep), out_shape=(...]
where the time goes in v3:
time: 42.2 us; the launch traced here: 42 us
  Pallas kernels  41.3 us (98%)
  between operations  0.64 us (2%)
    pallas_call x1, Pallas kernels, fused_body(): pl.pallas_call(functools.partial(fused_kernel, n_seq, n_rep), out_shape=(...  40.7 us

profile of v3, /device:TPU:0, one launch (start us, length us, event | category | flops | bytes accessed | tf_op | source)
XLA Modules:
  0.0 42.0 jit_solution(12830261377337090129)
XLA Ops:
  0.6 40.7 %shard_map.165 = (bf16[16,1024]{1,0:T(8,128)(2,1)S(1)}, bf16[16,1024]{1,0:T(8,128)(2,1)S(1)}, bf16[16,512]{1,0:T(8,128)(2,1)S(1)}, bf16[16,512]{1,0:T(8,128)(2,1)S(1)}) custom-call(s32[4]{0:T(128)} %order_hbm.1, bf16[16,512]{1,0:T(8,128)(2,1)} %q_hbm.1, bf16[16,128]{1,0:T(8,128)(2,1)} %kn_hbm.1, bf16[16,128]{1,0:T(8,128)(2,1)} %vn_hbm.1, ...), custom_call_target="tpu_custom_call" | custom-call | tf_op jit(solution)/shard_map/pallas_call | solution.py:691
  41.3 0.7 %shard_map.166 = (bf16[16,1024]{1,0:T(8,128)(2,1)}, bf16[16,1024]{1,0:T(8,128)(2,1)}, bf16[16,512]{1,0:T(8,128)(2,1)}, bf16[16,512]{1,0:T(8,128)(2,1)}) custom-call(bf16[16,1024]{1,0:T(8,128)(2,1)S(1)} %get-tuple-element.8.refs_0_, bf16[16,1024]{1,0:T(8,128)(2,1)S(1)} %get-tuple-element.9.refs_1_, bf16[16,512]{1,0:T(8,128)(2,1)S(1)} %get-tuple-element.10.refs_2_, ...), custom_call_target="tpu_custom_call" | custom-call | tf_op jit(solution)/shard_map/pallas_call | solution.py:771

commit v4 on v3

--- a/solution.py
+++ b/solution.py
@@ -602,37 +602,41 @@
     mine_second = (idall[:, 1:2] == (rep % experts).astype(F32)).astype(F32)
     weight = share * mine_first + (1.0 - share) * mine_second
 
-    def weighted(to_chip, to_core, at, size):
-        start = (to_chip * 2 + to_core) * feat + at
-        cols = pl.ds(pl.multiple_of(start, size), size)
+    def weighted(to, at, size):
+        cols = pl.ds(pl.multiple_of(to * feat + at, size), size)
         return jnp.dot(hidden[...], wdown[:, cols], preferred_element_type=F32) * weight
 
-    def cross(j, h, parts):
+    def cross(to_chip, h, parts):
         size = feat // parts
         cols = pl.ds(h * size, size)
-        ysend[j, :, cols] = weighted(lax.rem(chip + j, chips), 1 - core, h * size, size).astype(BF16)
-        send(ysend.at[j, :, cols], yall.at[j, :, cols], y_rsem.at[j, h], seq, partner)
-
-    def keep(j, h, parts):
+        view = yall.at[to_chip, :, cols]
+        ysend[to_chip, :, cols] = weighted(to_chip * 2 + 1 - core, h * size, size).astype(BF16)
+        send(ysend.at[to_chip, :, cols], view, y_rsem.at[to_chip, h], seq, partner)
+
+    def keep(to_chip, h, parts):
         size = feat // parts
         cols = pl.ds(h * size, size)
-        product = weighted(lax.rem(chip + j, chips), core, h * size, size)
-        view = yall.at[j, :, cols]
-        remote(view, view, send_sem, y_rsem.at[j, h], seq, partner).wait_recv()
-        psend[j, :, cols] = (product + yall[j, :, cols].astype(F32)).astype(BF16)
-        owner = lax.rem(chip + j, chips) * 2 + core
-        for to in far_first + [seq] * min(j, 1):
-            place = fin_all.at[seq, chip, :, cols]
-            send(psend.at[j, rows_of(to), cols], place, z_rsem.at[seq, chip], to, owner)
-
-    for j in range(1, chips):
-        for h in range(HALF):
-            cross(j, h, HALF)
-    for j in range(1, chips):
-        for h in range(HALF):
-            keep(j, h, HALF)
-    cross(0, 0, 1)
-    keep(0, 0, 1)
+        owner = to_chip * 2 + core
+        product = weighted(owner, h * size, size)
+        view = yall.at[to_chip, :, cols]
+        remote(view, view, send_sem, y_rsem.at[to_chip, h], seq, partner).wait_recv()
+        psend[to_chip, :, cols] = (product + yall[to_chip, :, cols].astype(F32)).astype(BF16)
+        place = fin_all.at[seq, chip, :, cols]
+        for to in far_first:
+            send(psend.at[to_chip, rows_of(to), cols], place, z_rsem.at[seq, chip], to, owner)
+
+        @pl.when(chip != to_chip)
+        def _():
+            block = psend.at[to_chip, mine, cols]
+            remote(block, place, send_sem, z_rsem.at[seq, chip], seq, owner).start()
+
+    sent[0] += (chips - 1) * tok * feat * 2
+    for to_chip in range(chips):
+        parts = 1 if to_chip else HALF
+        for h in range(parts):
+            cross(to_chip, h, parts)
+        for h in range(parts):
+            keep(to_chip, h, parts)
 
     wait_all(cache_rsem, 2 * (n_rep - 1) * size_of(kn_ref))
     kc_out[...] = kcache[...]
@@ -640,7 +644,7 @@
     wait_all(cache_ssem, 2 * (n_rep - 1) * size_of(kn_ref))
     wait_all(send_sem, sent[0])
 
-    result = att_out[...].astype(F32) + psend[0, mine, :].astype(F32)
+    result = att_out[...].astype(F32) + psend[chip, mine, :].astype(F32)
     for frm_s, frm_chip in [(seq, lax.rem(chip + j, chips)) for j in range(1, chips)] + [
         (s, lax.rem(chip + j, chips)) for s in arrivals for j in range(chips)
     ]:

time: 42.2 us -> 40.7 us (0.964)
  Pallas kernels: 41.3 us -> 39.6 us
    pallas_call x1, Pallas kernels: 40.7 us -> 38.9 us  [fused_body(): pl.pallas_call(functools.partial(fused_kernel, n_seq, n_rep), out_shape=(...]
where the time goes in v4:
time: 40.7 us; the launch traced here: 40.2 us
  Pallas kernels  39.6 us (97%)
  between operations  0.64 us (2%)
    pallas_call x1, Pallas kernels, fused_body(): pl.pallas_call(functools.partial(fused_kernel, n_seq, n_rep), out_shape=(...  38.9 us

profile of v4, /device:TPU:0, one launch (start us, length us, event | category | flops | bytes accessed | tf_op | source)
XLA Modules:
  0.0 40.2 jit_solution(16739376413653103379)
XLA Ops:
  0.6 38.9 %shard_map.165 = (bf16[16,1024]{1,0:T(8,128)(2,1)S(1)}, bf16[16,1024]{1,0:T(8,128)(2,1)S(1)}, bf16[16,512]{1,0:T(8,128)(2,1)S(1)}, bf16[16,512]{1,0:T(8,128)(2,1)S(1)}) custom-call(s32[4]{0:T(128)} %order_hbm.1, bf16[16,512]{1,0:T(8,128)(2,1)} %q_hbm.1, bf16[16,128]{1,0:T(8,128)(2,1)} %kn_hbm.1, bf16[16,128]{1,0:T(8,128)(2,1)} %vn_hbm.1, ...), custom_call_target="tpu_custom_call" | custom-call | tf_op jit(solution)/shard_map/pallas_call | solution.py:695
  39.6 0.7 %shard_map.166 = (bf16[16,1024]{1,0:T(8,128)(2,1)}, bf16[16,1024]{1,0:T(8,128)(2,1)}, bf16[16,512]{1,0:T(8,128)(2,1)}, bf16[16,512]{1,0:T(8,128)(2,1)}) custom-call(bf16[16,1024]{1,0:T(8,128)(2,1)S(1)} %get-tuple-element.8.refs_0_, bf16[16,1024]{1,0:T(8,128)(2,1)S(1)} %get-tuple-element.9.refs_1_, bf16[16,512]{1,0:T(8,128)(2,1)S(1)} %get-tuple-element.10.refs_2_, ...), custom_call_target="tpu_custom_call" | custom-call | tf_op jit(solution)/shard_map/pallas_call | solution.py:775

commit v5 on v4

--- a/solution.py
+++ b/solution.py
@@ -415,16 +415,16 @@
 
     wait_all(num_rsem, (n_seq - 1) * size_of(num_send.at[0]))
 
-    lines = []
-    for i in range(n_seq):
-        coded = num_all[i, span:, :].astype(F32)
-        lines.append(coded[0:1] + coded[1:2] + coded[2:3])
-    lines.append(jnp.zeros((128 - n_seq, 2 * span), F32))
-    stat_cols = jnp.concatenate(lines, axis=0).T
-    highs = [stat_cols[:span, i : i + 1] for i in range(n_seq)]
+    ones = jnp.where(lax.broadcasted_iota(jnp.int32, (stat_rows, hd), 0) < 3, 1.0, 0.0).astype(BF16)
+    tn = (((0,), (0,)), ((), ()))
+    stat_cols = [
+        lax.dot_general(num_all[i, span:, :], ones, tn, preferred_element_type=F32)
+        for i in range(n_seq)
+    ]
+    highs = [cols[:span] for cols in stat_cols]
     top = functools.reduce(jnp.maximum, highs)
     scales = [jnp.exp(h - top) for h in highs]
-    full = sum(scales[i] * stat_cols[span:, i : i + 1] for i in range(n_seq))
+    full = sum(scales[i] * stat_cols[i][span:] for i in range(n_seq))
     heads = sum(scales[i] * num_all[i, :span, :].astype(F32) for i in range(n_seq)) / full
     head_send[...] = heads.astype(BF16)
 

time: 40.7 us -> 40.5 us (level)
  no operation moved by 1% of the time
where the time goes in v5:
time: 40.5 us; the launch traced here: 40.1 us
  Pallas kernels  39.4 us (97%)
  between operations  0.64 us (2%)
    pallas_call x1, Pallas kernels, fused_body(): pl.pallas_call(functools.partial(fused_kernel, n_seq, n_rep), out_shape=(...  38.7 us

profile of v5, /device:TPU:0, one launch (start us, length us, event | category | flops | bytes accessed | tf_op | source)
XLA Modules:
  0.0 40.1 jit_solution(1098429252783054887)
XLA Ops:
  0.6 38.7 %shard_map.165 = (bf16[16,1024]{1,0:T(8,128)(2,1)S(1)}, bf16[16,1024]{1,0:T(8,128)(2,1)S(1)}, bf16[16,512]{1,0:T(8,128)(2,1)S(1)}, bf16[16,512]{1,0:T(8,128)(2,1)S(1)}) custom-call(s32[4]{0:T(128)} %order_hbm.1, bf16[16,512]{1,0:T(8,128)(2,1)} %q_hbm.1, bf16[16,128]{1,0:T(8,128)(2,1)} %kn_hbm.1, bf16[16,128]{1,0:T(8,128)(2,1)} %vn_hbm.1, ...), custom_call_target="tpu_custom_call" | custom-call | tf_op jit(solution)/shard_map/pallas_call | solution.py:695
  39.4 0.7 %shard_map.166 = (bf16[16,1024]{1,0:T(8,128)(2,1)}, bf16[16,1024]{1,0:T(8,128)(2,1)}, bf16[16,512]{1,0:T(8,128)(2,1)}, bf16[16,512]{1,0:T(8,128)(2,1)}) custom-call(bf16[16,1024]{1,0:T(8,128)(2,1)S(1)} %get-tuple-element.8.refs_0_, bf16[16,1024]{1,0:T(8,128)(2,1)S(1)} %get-tuple-element.9.refs_1_, bf16[16,512]{1,0:T(8,128)(2,1)S(1)} %get-tuple-element.10.refs_2_, ...), custom_call_target="tpu_custom_call" | custom-call | tf_op jit(solution)/shard_map/pallas_call | solution.py:775
